TPU v7x, 64 devices: a 2x2x8 block of a 4x4x8 slice. The times are simulated.
64 devices in a mesh: replica: 4 (over x, y), pool: 16 (over z, core).
Axes of the slice: x: 2, y: 2, z: 8, core: 2. Of those that a mesh axis runs over, the one named last changes fastest.
The devices are a block of a 4x4x8 slice.
Arguments:
- pool: bfloat16 [2, 2048, 2, 256, 2, 128], P(None, ('replica', 'pool')), parts along dimension 1
- page_idx: int32 [16, 64, 4], P(None, ('replica', 'pool')), parts along dimension 1
- count: int32 [64, 16], P(('replica', 'pool')), parts along dimension 0
- x: bfloat16 [64, 64, 2048], P(('replica', 'pool')), parts along dimension 0
- norm_attn: bfloat16 [2, 2048], replicated
- wq: bfloat16 [2, 2048, 2048], replicated
- wk: bfloat16 [2, 2048, 256], replicated
- wv: bfloat16 [2, 2048, 256], replicated
- wo: bfloat16 [2, 2048, 2048], replicated
- norm_mlp: bfloat16 [2, 2048], replicated
- w_gate: bfloat16 [2, 2048, 11008], replicated
- w_up: bfloat16 [2, 2048, 11008], replicated
- w_down: bfloat16 [2, 11008, 2048], replicated
Outputs:
- output: bfloat16 [64, 64, 2048], P(('replica', 'pool')), parts along dimension 0
There are 4 independent parts. A program takes and returns all parts, laid end to end along the dimension named above; an argument that names none is the same for every part.
All inputs are finite; a program needn't handle non-finite values.
Results may differ from a plain program's by a relative error of at most 0.0156482.
Values are sent between devices in bfloat16 or wider.
A program may use at most 768 MiB of HBM per device.

v0:
```python
import jax
import jax.numpy as jnp
from jax import lax
from jax.sharding import PartitionSpec as P

EPS = 1e-5
ROPE_BASE = 500000.0


def rms_norm(vals, gain):
    vals_f = vals.astype(jnp.float32)
    inv_rms = lax.rsqrt(jnp.mean(vals_f * vals_f, axis=-1, keepdims=True) + EPS)
    return (vals_f * inv_rms * gain.astype(jnp.float32)).astype(jnp.bfloat16)


def rotate(proj, tokens):
    half = proj.shape[-1] // 2
    freqs = ROPE_BASE ** (-jnp.arange(half, dtype=jnp.float32) / half)
    angles = jnp.arange(tokens, dtype=jnp.float32)[:, None] * freqs[None, :]
    cos_t = jnp.cos(angles)[:, None, :]
    sin_t = jnp.sin(angles)[:, None, :]
    first = proj[..., :half]
    second = proj[..., half:]
    return jnp.concatenate([first * cos_t - second * sin_t, second * cos_t + first * sin_t], axis=-1)


def decoder_layer(x_req, incoming, pre_ok, causal, weights):
    g_attn, wq_l, wk_l, wv_l, wo_l, g_mlp, wg_l, wu_l, wd_l = weights
    tokens = x_req.shape[0]
    kv_heads, head_dim = incoming.shape[4], incoming.shape[5]
    heads = wq_l.shape[1] // head_dim
    scale = head_dim ** -0.5
    h_attn = rms_norm(x_req, g_attn)
    q_proj = jnp.dot(h_attn, wq_l, preferred_element_type=jnp.float32).reshape(tokens, heads, head_dim)
    k_proj = jnp.dot(h_attn, wk_l, preferred_element_type=jnp.float32).reshape(tokens, kv_heads, head_dim)
    q_group = rotate(q_proj, tokens).astype(jnp.bfloat16).reshape(tokens, kv_heads, heads // kv_heads, head_dim)
    k_new = rotate(k_proj, tokens).astype(jnp.bfloat16)
    v_new = jnp.dot(h_attn, wv_l, preferred_element_type=jnp.float32).astype(jnp.bfloat16).reshape(tokens, kv_heads, head_dim)
    k_pre = incoming[:, :, 0]
    v_pre = incoming[:, :, 1]
    score_pre = jnp.einsum('tgrd,oksgd->grtoks', q_group, k_pre, preferred_element_type=jnp.float32) * scale
    score_pre = jnp.where(pre_ok, score_pre, -1e30)
    score_new = jnp.einsum('tgrd,ugd->grtu', q_group, k_new, preferred_element_type=jnp.float32) * scale
    score_new = jnp.where(causal, score_new, -1e30)
    peak = jnp.maximum(jnp.max(score_pre, axis=(3, 4, 5)), jnp.max(score_new, axis=3))
    exp_pre = jnp.exp(score_pre - peak[:, :, :, None, None, None])
    exp_new = jnp.exp(score_new - peak[:, :, :, None])
    inv_total = 1.0 / (jnp.sum(exp_pre, axis=(3, 4, 5)) + jnp.sum(exp_new, axis=3))
    prob_pre = (exp_pre * inv_total[:, :, :, None, None, None]).astype(jnp.bfloat16)
    prob_new = (exp_new * inv_total[:, :, :, None]).astype(jnp.bfloat16)
    attn_sum = jnp.einsum('grtoks,oksgd->tgrd', prob_pre, v_pre, preferred_element_type=jnp.float32) + jnp.einsum('grtu,ugd->tgrd', prob_new, v_new, preferred_element_type=jnp.float32)
    attn = attn_sum.astype(jnp.bfloat16).reshape(tokens, heads * head_dim)
    x_mid = (x_req.astype(jnp.float32) + jnp.dot(attn, wo_l, preferred_element_type=jnp.float32)).astype(jnp.bfloat16)
    h_mlp = rms_norm(x_mid, g_mlp)
    gate = jnp.dot(h_mlp, wg_l, preferred_element_type=jnp.float32)
    up_proj = jnp.dot(h_mlp, wu_l, preferred_element_type=jnp.float32)
    gated = (jax.nn.silu(gate) * up_proj).astype(jnp.bfloat16)
    return (x_mid.astype(jnp.float32) + jnp.dot(gated, wd_l, preferred_element_type=jnp.float32)).astype(jnp.bfloat16)


def solution(mesh):
    group = mesh.shape['pool']
    by_request = P(('replica', 'pool'))
    by_owner = P(None, ('replica', 'pool'))
    shared = P()

    def per_device(pool_loc, idx_loc, count_loc, x_loc, norm_attn, wq, wk, wv, wo, norm_mlp, w_gate, w_up, w_down):
        layers = pool_loc.shape[0]
        page_len, kv_heads, head_dim = pool_loc.shape[3], pool_loc.shape[4], pool_loc.shape[5]
        slots = idx_loc.shape[2]
        tokens = x_loc.shape[1]
        send_rows = idx_loc.reshape(group * slots)
        slot_ok = jnp.arange(slots)[None, :] < count_loc[0][:, None]
        pre_ok = jnp.broadcast_to(slot_ok[:, :, None], (group, slots, page_len))
        causal = jnp.arange(tokens)[None, :] <= jnp.arange(tokens)[:, None]
        x_req = x_loc[0]
        for layer in range(layers):
            outgoing = jnp.take(pool_loc[layer], send_rows, axis=0).reshape(group, slots, 2, page_len, kv_heads, head_dim)
            incoming = lax.all_to_all(outgoing, 'pool', 0, 0, tiled=True)
            weights = (norm_attn[layer], wq[layer], wk[layer], wv[layer], wo[layer], norm_mlp[layer], w_gate[layer], w_up[layer], w_down[layer])
            x_req = decoder_layer(x_req, incoming, pre_ok, causal, weights)
        return x_req[None]

    return jax.shard_map(per_device, mesh=mesh, in_specs=(by_owner, by_owner, by_request, by_request, shared, shared, shared, shared, shared, shared, shared, shared, shared), out_specs=by_request, check_vma=False)
```

profile of v0, /device:TPU:21, one launch (start us, length us, event | category | flops | bytes accessed | tf_op | source)
XLA Modules:
  0.0 985.0 jit_solution(4293016794893354246)
XLA Ops:
  0.0 0.8 copy.82
  0.8 0.1 reshape.229
  0.9 13.1 %fusion.141 = (bf16[1,32,2,256,2,128]{5,4,3,2,1,0:T(2,128)(2,1)S(1)}, bf16[1,32,2,256,2,128]{5,4,3,2,1,0:T(2,128)(2,1)S(1)}) fusion(bf16[2,32,2,256,2,128]{5,4,3,2,1,0:T(2,128)(2,1)} %param.15), kind=kLoop, calls=%fused_computation.171 | loop fusion | bytes 33554432 | tf_op jit(solution)/shard_map/slice | solution.py:78
  14.0 7.5 copy_bitcast_fusion.4
  21.5 11.0 %gather_fusion.1 = bf16[64,2,256,2,128]{4,2,3,1,0:T(8,128)(2,1)} fusion(bf16[32,2,256,2,128]{4,2,3,1,0:T(8,128)(2,1)} %get-tuple-element.46, s32[1024]{0:T(1024)S(1)} %pad_clamp_fusion), kind=kCustom, calls=%fused_computation.1.clone | custom fusion | bytes 33554688 | tf_op jit(solution)/shard_map/jit(_take)/gather | solution.py:78
  32.4 11.0 %gather_fusion = bf16[64,2,256,2,128]{4,2,3,1,0:T(8,128)(2,1)} fusion(bf16[32,2,256,2,128]{4,2,3,1,0:T(8,128)(2,1)} %get-tuple-element.47, s32[1024]{0:T(1024)S(1)} %pad_clamp_fusion), kind=kCustom, calls=%fused_computation.clone | custom fusion | bytes 33554688 | tf_op jit(solution)/shard_map/jit(_take)/gather | solution.py:78
  43.4 18.0 %broadcast_select_fusion = (bf16[64,2,256,2,128]{4,2,3,1,0:T(8,128)(2,1)}, bf16[64,2,256,2,128]{4,2,3,1,0:T(8,128)(2,1)S(1)}) fusion(bf16[64,2,256,2,128]{4,2,3,1,0:T(8,128)(2,1)} %gather_fusion.1, pred[64]{0:T(512)(128)(4,1)S(1)} %compare_and_fusion, bf16[64,2,256,2,128]{4,2,3,1,0:T(8,128)(2,1)} %gather_fusion), kind=kLoop, calls=%fused_computation.36 | loop fusion | flops 16777216 | bytes 67108928 | tf_op jit(solution)/shard_map/jit(_take)/select_n | solution.py:78
  61.4 6.9 copy.84
  68.3 10.8 %all-to-all-start = ((bf16[16,4,2,256,2,128]{5,3,1,4,2,0:T(8,128)(2,1)}), bf16[16,4,2,256,2,128]{5,3,1,4,2,0:T(8,128)(2,1)}, u32[]{:S(2)}, u32[]{:S(2)}) async-start(bf16[16,4,2,256,2,128]{5,3,1,4,2,0:T(8,128)(2,1)} %copy.84), calls=%async_computation | async-start | bytes 33554432 | tf_op jit(solution)/shard_map/all_to_all | solution.py:79
  79.1 14.0 %copy.94 = bf16[16,4,2,256,2,128]{5,3,1,4,2,0:T(8,128)(2,1)} copy(bf16[16,4,2,256,2,128]{5,3,4,2,1,0:T(8,128)(2,1)} %bitcast.253) | data formatting | bytes 33554432 | tf_op jit(solution)/shard_map/reshape | solution.py:78
  93.1 365.7 %all-to-all-done = bf16[16,4,2,256,2,128]{5,3,1,4,2,0:T(8,128)(2,1)} async-done(((bf16[16,4,2,256,2,128]{5,3,1,4,2,0:T(8,128)(2,1)}), bf16[16,4,2,256,2,128]{5,3,1,4,2,0:T(8,128)(2,1)}, u32[]{:S(2)}, u32[]{:S(2)}) %all-to-all-start) | async-done | bytes 16777248 | tf_op jit(solution)/shard_map/all_to_all | solution.py:79
  458.8 7.4 all-to-all-start.1
  466.3 11.8 %slice_bitcast_fusion = (bf16[2048,2048]{0,1:T(8,128)(2,1)}, bf16[2048,2048]{0,1:T(8,128)(2,1)}) fusion(bf16[2,2048,2048]{2,1,0:T(8,128)(2,1)} %param.20), kind=kLoop, calls=%fused_computation.55 | loop fusion | bytes 33554432 | tf_op jit(solution)/shard_map/dot_general | solution.py:34
  478.1 12.3 %copy.87 = bf16[2048,2048]{1,0:T(8,128)(2,1)} copy(bf16[2048,2048]{0,1:T(8,128)(2,1)} %get-tuple-element.9) | data formatting | bytes 16777216 | tf_op jit(solution)/shard_map/dot_general | solution.py:34
  490.4 1.7 slice_bitcast_fusion.2
  492.1 0.6 copy.88
  492.7 0.0 copy-done.1
  492.8 0.2 fusion.101
  492.9 0.6 slice_convert_fusion.1
  493.5 1.6 convolution_convert_fusion.1
  495.1 12.3 %copy.97 = bf16[2048,2048]{1,0:T(8,128)(2,1)} copy(bf16[2048,2048]{0,1:T(8,128)(2,1)} %get-tuple-element.8) | data formatting | bytes 16777216 | tf_op jit(solution)/shard_map/dot_general | solution.py:34
  507.5 1.4 copy.98
  508.9 0.0 copy-start.6
  509.0 0.1 iota_compare_fusion.1
  509.0 0.1 fusion.132
  509.2 0.0 copy-start.4
  509.2 0.4 fusion.116
  509.6 0.1 subtract_convert_fusion.3
  509.7 6.1 fusion.118
  515.8 0.3 subtract_convert_fusion.1
  516.1 0.5 fusion.143
  516.6 0.6 slice_convert_fusion
  517.2 9.5 fusion.142
  526.7 23.6 %bitcast_reduce_fusion.1 = (f32[2,8,64]{2,1,0:T(8,128)S(1)}, f32[2,16,4,256,64,8]{3,4,5,2,1,0:T(8,128)}) fusion(pred[16,4]{1,0:T(8,128)(4,1)S(1)} %iota_compare_fusion.1, bf16[64,2,8,64]{3,0,2,1:T(8,128)(2,1)S(1)} %bitcast.266, bf16[64,2,8,64]{3,0,2,1:T(8,128)(2,1)S(1)} %bitcast.264, bf16[16,4,1,256,2,128]{5,3,1,4,2,0:T(8,128)(2,1)S(1)} %get-tuple-element.13), kind=kOutput, calls=%fused_computation.6 | convolution fusion | flops 4345822208 | bytes 75763776 | tf_op jit(solution)/shard_map/tgrd,oksgd->grtoks/dot_general | solution.py:41
  550.2 0.1 fusion.104
  550.4 21.4 %fusion.2 = f32[2,8,64]{2,1,0:T(8,128)S(1)} fusion(f32[2,16,4,256,64,8]{3,4,5,2,1,0:T(8,128)} %get-tuple-element.33, f32[2,8,64]{2,1,0:T(8,128)S(1)} %max.22, pred[16,4]{1,0:T(8,128)(4,1)S(1)} %iota_compare_fusion.1), kind=kLoop, calls=%fused_computation.12 | loop fusion | flops 67107840 | bytes 67117120 | tf_op jit(solution)/shard_map/reduce_sum | solution.py:48
  571.8 26.6 %fusion.86 = f32[2,128,8,64]{1,3,2,0:T(8,128)S(1)} fusion(bf16[16,4,1,256,2,128]{5,3,1,4,2,0:T(8,128)(2,1)} %get-tuple-element.12, f32[2,16,4,256,64,8]{3,4,5,2,1,0:T(8,128)} %get-tuple-element.33, f32[2,8,64]{2,1,0:T(8,128)S(1)} %add_divide_fusion.1, f32[2,8,64]{2,1,0:T(8,128)S(1)} %max.22, pred[16,4]{1,0:T(8,128)(4,1)S(1)} %iota_compare_fusion.1), kind=kOutput, calls=%fused_computation.78 | convolution fusion | flops 4378853376 | bytes 76030016 | tf_op jit(solution)/shard_map/grtoks,oksgd->tgrd/dot_general | solution.py:51
  598.4 0.3 fusion.95
  598.7 0.2 copy.92
  598.9 5.1 multiply_reduce_fusion.2
  604.0 16.9 %fusion.14 = f32[64,11008]{1,0:T(8,128)S(1)} fusion(bf16[2,2048,11008]{2,1,0:T(8,128)(2,1)} %param.25, f32[64,2048]{1,0:T(8,128)S(1)} %get-tuple-element.37, f32[2048]{0:T(1024)S(1)} %bitcast.277, f32[64]{0:T(128)S(1)} %add_rsqrt_fusion.2), kind=kOutput, calls=%fused_computation.24 | convolution fusion | flops 2886074368 | bytes 48439552 | tf_op jit(solution)/shard_map/dot_general | solution.py:55
  620.9 17.0 %fusion.35 = bf16[64,11008]{1,0:T(8,128)(2,1)S(1)} fusion(bf16[2,2048,11008]{2,1,0:T(8,128)(2,1)} %param.26, f32[64,11008]{1,0:T(8,128)S(1)} %fusion.14, f32[64,2048]{1,0:T(8,128)S(1)} %get-tuple-element.37, f32[2048]{0:T(1024)S(1)} %bitcast.278, f32[64]{0:T(128)S(1)} %add_rsqrt_fusion.2), kind=kOutput, calls=%fused_computation.41 | convolution fusion | flops 2890301440 | bytes 49848576 | tf_op jit(solution)/shard_map/dot_general | solution.py:56
  637.9 0.0 copy-start.5
  638.0 0.0 copy-start.13
  638.0 17.4 %multiply_reduce_fusion.1 = (f32[64]{0:T(128)S(1)}, f32[64,2048]{1,0:T(8,128)S(1)}) fusion(f32[64,2048]{1,0:T(8,128)S(1)} %get-tuple-element.37, bf16[64,11008]{1,0:T(8,128)(2,1)S(1)} %fusion.35, bf16[2,11008,2048]{2,1,0:T(8,128)(2,1)} %param.27), kind=kOutput, calls=%fused_computation.105 | convolution fusion | flops 2886336512 | bytes 47546624 | tf_op jit(solution)/shard_map/dot_general | solution.py:58
  655.4 0.1 multiply_convert_fusion.4
  655.6 0.4 fusion.112
  656.0 0.1 subtract_convert_fusion.2
  656.1 6.0 fusion.114
  662.2 0.3 subtract_convert_fusion
  662.4 0.3 convolution_convert_fusion
  662.7 182.9 %all-to-all-done.1 = bf16[16,4,2,256,2,128]{5,3,1,4,2,0:T(8,128)(2,1)} async-done(((bf16[16,4,2,256,2,128]{5,3,1,4,2,0:T(8,128)(2,1)}), bf16[16,4,2,256,2,128]{5,3,1,4,2,0:T(8,128)(2,1)}, u32[]{:S(2)}, u32[]{:S(2)}) %all-to-all-start.1) | async-done | bytes 16777248 | tf_op jit(solution)/shard_map/all_to_all | solution.py:79
  845.6 9.5 fusion.140
  855.1 23.6 %bitcast_reduce_fusion = (f32[2,8,64]{2,1,0:T(8,128)S(1)}, f32[2,16,4,256,64,8]{3,4,5,2,1,0:T(8,128)}) fusion(pred[16,4]{1,0:T(8,128)(4,1)S(1)} %iota_compare_fusion.1, bf16[64,2,8,64]{3,0,2,1:T(8,128)(2,1)S(1)} %bitcast.261, bf16[64,2,8,64]{3,0,2,1:T(8,128)(2,1)S(1)} %bitcast.259, bf16[16,4,1,256,2,128]{5,3,1,4,2,0:T(8,128)(2,1)S(1)} %get-tuple-element.7), kind=kOutput, calls=%fused_computation.3 | convolution fusion | flops 4345822208 | bytes 75763776 | tf_op jit(solution)/shard_map/tgrd,oksgd->grtoks/dot_general | solution.py:41
  878.7 0.5 fusion.144
  879.2 21.4 %fusion.3 = f32[2,8,64]{2,1,0:T(8,128)S(1)} fusion(f32[2,16,4,256,64,8]{3,4,5,2,1,0:T(8,128)} %get-tuple-element.41, f32[2,8,64]{2,1,0:T(8,128)S(1)} %max.23, pred[16,4]{1,0:T(8,128)(4,1)S(1)} %iota_compare_fusion.1), kind=kLoop, calls=%fused_computation.13 | loop fusion | flops 67107840 | bytes 67117120 | tf_op jit(solution)/shard_map/reduce_sum | solution.py:48
  900.5 0.1 fusion.105
  900.7 26.7 %fusion.89 = f32[2,128,8,64]{1,3,2,0:T(8,128)S(1)} fusion(bf16[16,4,1,256,2,128]{5,3,1,4,2,0:T(8,128)(2,1)} %get-tuple-element.6, f32[2,16,4,256,64,8]{3,4,5,2,1,0:T(8,128)} %get-tuple-element.41, f32[2,8,64]{2,1,0:T(8,128)S(1)} %add_divide_fusion, f32[2,8,64]{2,1,0:T(8,128)S(1)} %max.23, pred[16,4]{1,0:T(8,128)(4,1)S(1)} %iota_compare_fusion.1), kind=kOutput, calls=%fused_computation.79 | convolution fusion | flops 4378853376 | bytes 76030016 | tf_op jit(solution)/shard_map/grtoks,oksgd->tgrd/dot_general | solution.py:51
  927.4 0.3 fusion.94
  927.7 0.2 copy.102
  927.9 5.1 multiply_reduce_fusion
  933.0 16.9 %fusion.8 = f32[64,11008]{1,0:T(8,128)S(1)} fusion(bf16[2,2048,11008]{2,1,0:T(8,128)(2,1)} %param.25, f32[64,2048]{1,0:T(8,128)S(1)} %get-tuple-element.45, f32[2048]{0:T(1024)S(1)} %bitcast.275, f32[64]{0:T(128)S(1)} %add_rsqrt_fusion), kind=kOutput, calls=%fused_computation.18 | convolution fusion | flops 2886074368 | bytes 48439552 | tf_op jit(solution)/shard_map/dot_general | solution.py:55
  950.0 17.0 %fusion.32 = bf16[64,11008]{1,0:T(8,128)(2,1)S(1)} fusion(bf16[2,2048,11008]{2,1,0:T(8,128)(2,1)} %param.26, f32[64,11008]{1,0:T(8,128)S(1)} %fusion.8, f32[64,2048]{1,0:T(8,128)S(1)} %get-tuple-element.45, f32[2048]{0:T(1024)S(1)} %bitcast.276, f32[64]{0:T(128)S(1)} %add_rsqrt_fusion), kind=kOutput, calls=%fused_computation.40 | convolution fusion | flops 2890301440 | bytes 49848576 | tf_op jit(solution)/shard_map/dot_general | solution.py:56
  967.0 17.7 %fusion.79 = bf16[1,64,2048]{2,1,0:T(8,128)(2,1)} fusion(f32[64,2048]{1,0:T(8,128)S(1)} %get-tuple-element.45, bf16[64,11008]{1,0:T(8,128)(2,1)S(1)} %fusion.32, bf16[2,11008,2048]{2,1,0:T(8,128)(2,1)} %param.27), kind=kOutput, calls=%fused_computation.69 | convolution fusion | flops 2885943296 | bytes 47284224 | tf_op jit(solution)/shard_map/dot_general | solution.py:58
  (38 shorter events, 0.2 us)
Async XLA Ops:
  68.3 390.5 %all-to-all-start = ((bf16[16,4,2,256,2,128]{5,3,1,4,2,0:T(8,128)(2,1)}), bf16[16,4,2,256,2,128]{5,3,1,4,2,0:T(8,128)(2,1)}, u32[]{:S(2)}, u32[]{:S(2)}) async-start(bf16[16,4,2,256,2,128]{5,3,1,4,2,0:T(8,128)(2,1)} %copy.84), calls=%async_computation | async-start | bytes 33554432 | tf_op jit(solution)/shard_map/all_to_all | solution.py:79
  458.8 386.8 %all-to-all-start.1 = ((bf16[16,4,2,256,2,128]{5,3,1,4,2,0:T(8,128)(2,1)}), bf16[16,4,2,256,2,128]{5,3,1,4,2,0:T(8,128)(2,1)}, u32[]{:S(2)}, u32[]{:S(2)}) async-start(bf16[16,4,2,256,2,128]{5,3,1,4,2,0:T(8,128)(2,1)} %copy.94), calls=%async_computation.1 | async-start | bytes 33554432 | tf_op jit(solution)/shard_map/all_to_all | solution.py:79
  478.1 14.7 %copy-start.1 = (bf16[1,64,2048]{2,1,0:T(8,128)(2,1)S(1)}, bf16[1,64,2048]{2,1,0:T(8,128)(2,1)}, u32[]{:S(2)}) copy-start(bf16[1,64,2048]{2,1,0:T(8,128)(2,1)} %param.18) | copy-start | bytes 786436
  478.1 14.8 %copy-start.9 = (bf16[2,2048]{1,0:T(2,128)(2,1)S(1)}, bf16[2,2048]{1,0:T(2,128)(2,1)}, u32[]{:S(2)}) copy-start(bf16[2,2048]{1,0:T(2,128)(2,1)} %param.19) | copy-start | bytes 24580
  490.4 18.6 %copy-start.12 = (s32[1,16]{1,0:T(1,128)S(1)}, s32[1,16]{1,0:T(1,128)}, u32[]{:S(2)}) copy-start(s32[1,16]{1,0:T(1,128)} %param.17) | copy-start | bytes 196
  493.5 23.0 %copy-start.10 = (bf16[2,2048]{1,0:T(2,128)(2,1)S(1)}, bf16[2,2048]{1,0:T(2,128)(2,1)}, u32[]{:S(2)}) copy-start(bf16[2,2048]{1,0:T(2,128)(2,1)} %param.24) | copy-start | bytes 24580
  508.9 17.7 %copy-start.6 = (pred[64,64]{0,1:T(8,128)(4,1)}, pred[64,64]{0,1:T(8,128)(4,1)S(1)}, u32[]{:S(2)}) copy-start(pred[64,64]{0,1:T(8,128)(4,1)S(1)} %iota_compare_fusion) | copy-start | bytes 12292
  509.2 17.5 %copy-start.2 = (f32[64,64]{1,0:T(8,128)}, f32[64,64]{1,0:T(8,128)S(1)}, u32[]{:S(2)}) copy-start(f32[64,64]{1,0:T(8,128)S(1)} %get-tuple-element.30) | copy-start | bytes 49156
  509.2 17.5 %copy-start.4 = (f32[64,64]{1,0:T(8,128)}, f32[64,64]{1,0:T(8,128)S(1)}, u32[]{:S(2)}) copy-start(f32[64,64]{1,0:T(8,128)S(1)} %get-tuple-element.31) | copy-start | bytes 49156
  637.9 17.5 %copy-start.8 = (f32[1,2048]{1,0:T(1,128)S(1)}, f32[1,2048]{1,0:T(1,128)}, u32[]{:S(2)}) copy-start(f32[1,2048]{1,0:T(1,128)} %get-tuple-element.26) | copy-start | bytes 24580
  637.9 17.6 %copy-start = (bf16[256,2048]{1,0:T(8,128)(2,1)S(1)}, bf16[256,2048]{1,0:T(8,128)(2,1)}, u32[]{:S(2)}) copy-start(bf16[256,2048]{1,0:T(8,128)(2,1)} %copy.98) | copy-start | bytes 3145732
  637.9 18.1 %copy-start.3 = (f32[64,64]{1,0:T(8,128)S(1)}, f32[64,64]{1,0:T(8,128)}, u32[]{:S(2)}) copy-start(f32[64,64]{1,0:T(8,128)} %copy-done.2) | copy-start | bytes 49156
  637.9 18.1 %copy-start.5 = (f32[64,64]{1,0:T(8,128)S(1)}, f32[64,64]{1,0:T(8,128)}, u32[]{:S(2)}) copy-start(f32[64,64]{1,0:T(8,128)} %copy-done.4) | copy-start | bytes 49156
  638.0 24.5 %copy-start.13 = (bf16[2,2048,256]{2,1,0:T(8,128)(2,1)S(1)}, bf16[2,2048,256]{2,1,0:T(8,128)(2,1)}, u32[]{:S(2)}) copy-start(bf16[2,2048,256]{2,1,0:T(8,128)(2,1)} %param.22) | copy-start | bytes 6291460
  855.1 23.6 %copy-start.7 = (pred[64,64]{0,1:T(8,128)(4,1)S(1)}, pred[64,64]{0,1:T(8,128)(4,1)}, u32[]{:S(2)}) copy-start(pred[64,64]{0,1:T(8,128)(4,1)} %copy-done.6) | copy-start | bytes 12292
  900.7 32.3 %copy-start.11 = (f32[1,2048]{1,0:T(1,128)S(1)}, f32[1,2048]{1,0:T(1,128)}, u32[]{:S(2)}) copy-start(f32[1,2048]{1,0:T(1,128)} %get-tuple-element.24) | copy-start | bytes 24580
where the time goes:
time: 990 us; the launch traced here: 985 us
  waiting for transfers between devices  549 us (55%)
  matrix products  230 us (23%)
  local copies, waits for them, and re-layouts  124 us (13%)
  other arithmetic  63.6 us (6%)
  starting transfers between devices  18.2 us (2%)
    all_to_all x2, waiting for transfers between devices, per_device(): incoming = lax.all_to_all(outgoing, 'pool', 0, 0, tiled=True)  549 us
    dot_general x2, matrix products, decoder_layer(): jnp.einsum('grtoks,oksgd->tgrd', prob_pre, v_pre, preferred_element_type=...  53.3 us
    dot_general x2, matrix products, decoder_layer(): jnp.einsum('tgrd,oksgd->grtoks', q_group, k_pre, preferred_element_type=j...  47.1 us
    reduce_sum x2, other arithmetic, decoder_layer(): jnp.sum(exp_pre, axis=(3, 4, 5)) + jnp.sum(exp_new, axis=3)  42.8 us
    dot_general x3, local copies, waits for them, and re-layouts, decoder_layer(): jnp.dot(h_attn, wq_l, preferred_element_type=jnp.float32)  36.5 us
    dot_general x2, matrix products, decoder_layer(): jnp.dot(gated, wd_l, preferred_element_type=jnp.float32)  35.1 us
    dot_general x2, matrix products, decoder_layer(): up_proj = jnp.dot(h_mlp, wu_l, preferred_element_type=jnp.float32)  34 us
    dot_general x2, matrix products, decoder_layer(): gate = jnp.dot(h_mlp, wg_l, preferred_element_type=jnp.float32)  33.9 us
  transfers between devices with their start and end apart: 2, of which 2 were waited for; matrix products, arithmetic and copies ran while one was open for 21% of the time, Pallas kernels for 0%

commit v1 on v0

v1 whole, which is shorter than its diff:
```python
import functools

import jax
import jax.numpy as jnp
from jax import lax
from jax.experimental import pallas as pl
from jax.experimental.pallas import tpu as pltpu
from jax.sharding import PartitionSpec as P

EPS = 1e-5
ROPE_BASE = 500000.0
NEG = -1e30
LOG2E = 1.4426950408889634
CHUNK = 512
DOWN = 256
PAIRS = 3
DOWNS = 3


def rms_norm(vals_f, gain):
    inv_rms = lax.rsqrt(jnp.mean(vals_f * vals_f, axis=-1, keepdims=True) + EPS)
    return (vals_f * inv_rms * gain).astype(jnp.bfloat16)


def dot32(a, b):
    return jnp.dot(a, b, preferred_element_type=jnp.float32)


def kernel(dims, tab, x_ref, cos_ref, sin_ref, ga_ref, gm_ref, kp, vp, wq, wk, wv, wo, wg, wu, wd, out_ref,
           xs, hs, avec, us, qbuf, acc, kpg, vpg, knew, vnew, scores, sent, got, wqo, wkv, gu, dn,
           q_ss, q_rs, a_ss, a_rs, pg_ls, pg_ss, pg_rs, x_ss, x_rs, p_ss, p_rs, wq_s, wkv_s, gu_s, dn_s):
    group, slots = dims
    chips = group // 2
    layers, _, d_model = ga_ref.shape
    tokens = x_ref.shape[0]
    hd = kp.shape[-1]
    page = kp.shape[3]
    pages = kp.shape[2]
    width = wq.shape[2] // 2
    heads = width // hd
    part = tokens // 2
    rows = heads * part
    ff = wg.shape[2] // 2
    n_gu = -(-ff // CHUNK)
    n_dn = d_model // DOWN
    n_out = d_model // CHUNK
    scale = hd ** -0.5 * LOG2E

    me = lax.axis_index("pool")
    z = me // 2
    c = me % 2
    mate = me + 1 - 2 * c

    def along(b):
        delta = jnp.where(b < 2, 1, chips - 1)
        return lax.rem(z + delta, chips) * 2 + c

    def to(dev):
        return {"pool": dev}

    def q_hop(layer, s, b):
        return pltpu.make_async_remote_copy(
            src_ref=qbuf.at[layer, s, b], dst_ref=qbuf.at[layer, s + 1, b], send_sem=q_ss.at[layer, s, b], recv_sem=q_rs.at[layer, s + 1, b],
            device_id=to(along(b)), device_id_type=pl.DeviceIdType.MESH)

    def a_hop(layer, s, b):
        return pltpu.make_async_remote_copy(
            src_ref=acc.at[layer, s, b], dst_ref=acc.at[layer, s + 1, b], send_sem=a_ss.at[layer, s, b], recv_sem=a_rs.at[layer, s + 1, b],
            device_id=to(along(b)), device_id_type=pl.DeviceIdType.MESH)

    def page_local(layer, which):
        src, dst = (kp, kpg) if which == 0 else (vp, vpg)
        return pltpu.make_async_copy(src.at[layer, c], dst.at[c], pg_ls.at[layer, which])

    def page_remote(layer, which):
        src, dst = (kp, kpg) if which == 0 else (vp, vpg)
        return pltpu.make_async_remote_copy(
            src_ref=src.at[layer, 1 - c], dst_ref=dst.at[c], send_sem=pg_ss.at[layer, which], recv_sem=pg_rs.at[layer, which],
            device_id=to(mate), device_id_type=pl.DeviceIdType.MESH)

    def part_hop(layer, k, n, size):
        cols = pl.ds(pl.multiple_of(n * size, size), size)
        return pltpu.make_async_remote_copy(
            src_ref=sent.at[k, :, cols], dst_ref=got.at[k, :, cols], send_sem=p_ss.at[layer, k, n], recv_sem=p_rs.at[layer, k, n],
            device_id=to(mate), device_id_type=pl.DeviceIdType.MESH)

    def load_wq(layer):
        cols = pl.ds(pl.multiple_of(c * width, width), width)
        return [pltpu.make_async_copy(wq.at[layer, :, cols], wqo, wq_s.at[0])]

    def load_wkv(layer):
        cols = pl.ds(pl.multiple_of(c * hd, hd), hd)
        return [pltpu.make_async_copy(w.at[layer, :, cols], wkv.at[i], wkv_s.at[i]) for i, w in enumerate((wk, wv))]

    def load_wo(layer):
        line = pl.ds(pl.multiple_of(c * width, width), width)
        return [pltpu.make_async_copy(wo.at[layer, line, pl.ds(i * width, width)], wqo.at[pl.ds(i * width, width), :], wq_s.at[1 + i])
                for i in range(2)]

    def gu_start(i):
        return pl.multiple_of(jnp.minimum(i * CHUNK, ff - CHUNK), 128)

    def load_gu(layer, i, slot):
        cols = pl.ds(pl.multiple_of(c * ff + gu_start(i), 128), CHUNK)
        return [pltpu.make_async_copy(w.at[layer, :, cols], gu.at[slot, j], gu_s.at[slot, j]) for j, w in enumerate((wg, wu))]

    def load_dn(layer, i, slot):
        line = pl.ds(pl.multiple_of(c * ff, 128), ff)
        return [pltpu.make_async_copy(wd.at[layer, line, pl.ds(pl.multiple_of(i * DOWN, DOWN), DOWN)], dn.at[slot], dn_s.at[slot])]

    def go(copies):
        for one in copies:
            one.start()

    def done(copies):
        for one in copies:
            one.wait()

    barrier = pltpu.get_barrier_semaphore()
    for dev in (mate, along(0), along(2)):
        pl.semaphore_signal(barrier, inc=1, device_id=to(dev), device_id_type=pl.DeviceIdType.MESH)
    go(load_wq(0) + load_wkv(0))
    go([page_local(0, 0), page_local(0, 1)])
    pl.semaphore_wait(barrier, 3)

    own = pl.ds(pl.multiple_of(c * tokens, tokens), tokens)
    x_swap = pltpu.make_async_remote_copy(
        src_ref=x_ref, dst_ref=xs.at[own], send_sem=x_ss, recv_sem=x_rs, device_id=to(mate), device_id_type=pl.DeviceIdType.MESH)
    x_swap.start()
    go([page_remote(0, 0), page_remote(0, 1)])
    xs[own, :] = x_ref[...]
    for i in range(PAIRS):
        go(load_gu(0, i, i))
    for i in range(DOWNS):
        go(load_dn(0, i, i))
    x_swap.wait()

    def attend(q_t, req, extra):
        spots = [(o, j) for o in range(2) for j in range(slots)]
        valid, peaks = [], []
        for n, (o, j) in enumerate(spots):
            owner = 2 * z + o
            s = dot32(kpg[o, tab[owner, req * slots + j]], q_t)
            scores[n] = s
            ok = j < tab[req, group * slots + owner]
            valid.append(ok)
            peaks.append(jnp.where(ok, jnp.max(s, axis=0, keepdims=True) * scale, NEG))
        top = functools.reduce(jnp.maximum, peaks)
        if extra is not None:
            new_s = extra[0]
            top = jnp.maximum(top, jnp.max(new_s, axis=0, keepdims=True) * scale)
        total = jnp.zeros_like(top)
        out = jnp.zeros((hd, rows), jnp.float32)
        for n, (o, j) in enumerate(spots):
            owner = 2 * z + o
            shift = jnp.where(valid[n], -top, NEG)
            p = jnp.exp2(scores[n] * scale + shift)
            total = total + jnp.sum(p, axis=0, keepdims=True)
            out = out + dot32(vpg[o, tab[owner, req * slots + j]], p.astype(jnp.bfloat16))
        if extra is not None:
            p = jnp.exp2(new_s * scale - top)
            total = total + jnp.sum(p, axis=0, keepdims=True)
            out = out + dot32(extra[1], p.astype(jnp.bfloat16))
        return out, top, total

    def put_acc(layer, s, b, out, top, total):
        acc[layer, s, b, :hd, :] = out
        line = lax.broadcasted_iota(jnp.int32, (8, rows), 0)
        acc[layer, s, b, hd:hd + 8, :] = jnp.where(line == 0, top, total)

    def merge(layer, s, b, out, top, total):
        in_out, in_top, in_total = acc[layer, s, b, :hd, :], acc[layer, s, b, hd:hd + 1, :], acc[layer, s, b, hd + 1:hd + 2, :]
        best = jnp.maximum(top, in_top)
        fa, fb = jnp.exp2(in_top - best), jnp.exp2(top - best)
        return in_out * fa + out * fb, best, in_total * fa + total * fb

    def rope(vals):
        return vals * cos_ref[...] + pltpu.roll(vals, hd // 2, axis=1) * sin_ref[...]

    def layer_body(layer, carry):
        last = layer == layers - 1
        hs[...] = rms_norm(xs[...].astype(jnp.float32), ga_ref[layer])
        done(load_wkv(layer))
        k_all = rope(dot32(hs[...], wkv[0])).astype(jnp.bfloat16)
        v_all = dot32(hs[...], wkv[1])
        for i in range(2):
            knew[i] = k_all[i * tokens:(i + 1) * tokens]
            vnew[i] = v_all[i * tokens:(i + 1) * tokens].T.astype(jnp.bfloat16)
        done(load_wq(layer))
        for n in range(heads):
            q_head = rope(dot32(hs[...], wqo[:, n * hd:(n + 1) * hd])).astype(jnp.bfloat16)
            avec[:, n * hd:(n + 1) * hd] = q_head
        for b in range(4):
            lo = (b % 2) * tokens + (b // 2) * part
            q_rows = jnp.concatenate([avec[lo:lo + part, n * hd:(n + 1) * hd] for n in range(heads)], axis=0)
            qbuf[layer, 0, b] = q_rows.astype(jnp.float32).T.astype(jnp.bfloat16)
            q_hop(layer, 0, b).start()
        go(load_wo(layer))

        @pl.when(layer + 1 < layers)
        def _():
            go(load_wkv(layer + 1))

        for b in range(4):
            put_acc(layer, 1, b, jnp.zeros((hd, rows), jnp.float32), jnp.full((1, rows), NEG), jnp.zeros((1, rows), jnp.float32))
        for which in range(2):
            page_local(layer, which).wait()
            page_remote(layer, which).wait()

        def home(b, carry):
            i = lax.rem(b, 2)
            q_t = qbuf[layer, 0, b]
            s = dot32(knew[i], q_t)
            key = lax.broadcasted_iota(jnp.int32, s.shape, 0)
            tok = lax.rem(lax.broadcasted_iota(jnp.int32, s.shape, 1), part) + (b // 2) * part
            s = jnp.where(key <= tok, s, NEG)
            put_acc(layer, 0, b, *attend(q_t, 2 * z + i, (s, vnew[i])))
            return carry

        lax.fori_loop(0, 4, home, 0)

        def step(s, carry):
            for b in range(4):
                q_hop(layer, s - 1, b).wait_recv()

                @pl.when(s < chips - 1)
                def _():
                    q_hop(layer, s, b).start()

            def block(b, carry):
                source = lax.rem(z + jnp.where(b < 2, chips - s, s), chips)
                found = attend(qbuf[layer, s, b], 2 * source + lax.rem(b, 2), None)

                @pl.when(s >= 2)
                def _():
                    a_hop(layer, s - 1, b).wait_recv()

                put_acc(layer, s, b, *merge(layer, s, b, *found))
                a_hop(layer, s, b).start()
                return carry

            return lax.fori_loop(0, 4, block, carry)

        lax.fori_loop(1, chips, step, 0)

        for b in range(4):
            a_hop(layer, chips - 1, b).wait_recv()
            out, top, total = merge(layer, chips, b, acc[layer, 0, b, :hd, :], acc[layer, 0, b, hd:hd + 1, :], acc[layer, 0, b, hd + 1:hd + 2, :])
            a_rows = (out / total).T.astype(jnp.bfloat16)
            lo = (b % 2) * tokens + (b // 2) * part
            for n in range(heads):
                avec[lo:lo + part, n * hd:(n + 1) * hd] = a_rows[n * part:(n + 1) * part]

        def drain(s, carry):
            for b in range(4):
                q_hop(layer, s, b).wait_send()
                a_hop(layer, s + 1, b).wait_send()
            return carry

        lax.fori_loop(0, chips - 1, drain, 0)

        done(load_wo(layer))
        for n in range(n_out):
            half, off = divmod(n * CHUNK, width)
            sent[0, :, n * CHUNK:(n + 1) * CHUNK] = dot32(avec[...], wqo[half * width:(half + 1) * width, off:off + CHUNK])
            part_hop(layer, 0, n, CHUNK).start()

        @pl.when(layer + 1 < layers)
        def _():
            go(load_wq(layer + 1))

        for n in range(n_out):
            part_hop(layer, 0, n, CHUNK).wait()
        x_mid = (xs[...].astype(jnp.float32) + (sent[0] + got[0])).astype(jnp.bfloat16)
        xs[...] = x_mid

        @pl.when(layer + 1 < layers)
        def _():
            go([page_local(layer + 1, 0), page_local(layer + 1, 1), page_remote(layer + 1, 0), page_remote(layer + 1, 1)])

        hs[...] = rms_norm(xs[...].astype(jnp.float32), gm_ref[layer])

        def gate_up(i, carry):
            slot = lax.rem(layer * n_gu + i, PAIRS)
            done(load_gu(layer, i, slot))
            gate = dot32(hs[...], gu[slot, 0])
            up = dot32(hs[...], gu[slot, 1])
            us[:, pl.ds(gu_start(i), CHUNK)] = (gate * (1.0 / (1.0 + jnp.exp(-gate))) * up).astype(jnp.bfloat16)
            ahead = i + PAIRS

            @pl.when(ahead < n_gu)
            def _():
                go(load_gu(layer, ahead, slot))

            @pl.when(jnp.logical_and(ahead >= n_gu, layer + 1 < layers))
            def _():
                go(load_gu(layer + 1, ahead - n_gu, slot))

            return carry

        lax.fori_loop(0, n_gu, gate_up, 0)

        def down(i, carry):
            slot = lax.rem(layer * n_dn + i, DOWNS)
            done(load_dn(layer, i, slot))
            sent[1, :, pl.ds(pl.multiple_of(i * DOWN, DOWN), DOWN)] = dot32(us[...], dn[slot])
            part_hop(layer, 1, i, DOWN).start()
            ahead = i + DOWNS

            @pl.when(ahead < n_dn)
            def _():
                go(load_dn(layer, ahead, slot))

            @pl.when(jnp.logical_and(ahead >= n_dn, layer + 1 < layers))
            def _():
                go(load_dn(layer + 1, ahead - n_dn, slot))

            return carry

        lax.fori_loop(0, n_dn, down, 0)
        for n in range(n_dn):
            part_hop(layer, 1, n, DOWN).wait()
        xs[...] = (xs[...].astype(jnp.float32) + (sent[1] + got[1])).astype(jnp.bfloat16)
        return carry

    lax.fori_loop(0, layers, layer_body, 0)
    out_ref[...] = xs[own, :]


def solution(mesh):
    group = mesh.shape["pool"]
    by_request = P(("replica", "pool"))
    by_owner = P(None, ("replica", "pool"))
    shared = P()

    def per_device(pool_loc, idx_loc, count_loc, x_loc, norm_attn, wq, wk, wv, wo, norm_mlp, w_gate, w_up, w_down):
        layers, pages, _, page, kv_heads, hd = pool_loc.shape
        slots = idx_loc.shape[2]
        tokens, d_model = x_loc.shape[1:]
        chips = group // 2
        width = wq.shape[2] // 2
        heads = width // hd
        rows = heads * tokens // 2
        ff = w_gate.shape[2] // 2
        both = 2 * tokens

        table = lax.all_gather(jnp.concatenate([idx_loc.reshape(-1), count_loc.reshape(-1)]), "pool")
        k_pages = jnp.transpose(pool_loc[:, :, 0], (0, 3, 1, 2, 4))
        v_pages = jnp.transpose(pool_loc[:, :, 1], (0, 3, 1, 4, 2))
        half = hd // 2
        freqs = ROPE_BASE ** (-jnp.arange(half, dtype=jnp.float32) / half)
        angles = jnp.arange(tokens, dtype=jnp.float32)[:, None] * freqs[None, :]
        cos_t = jnp.tile(jnp.cos(angles), (2, 2))
        sin_t = jnp.tile(jnp.concatenate([-jnp.sin(angles), jnp.sin(angles)], axis=1), (2, 1))

        def gains(one):
            return one.astype(jnp.float32)[:, None]

        vmem = pl.BlockSpec(memory_space=pltpu.VMEM)
        smem = pl.BlockSpec(memory_space=pltpu.SMEM)
        hbm = pl.BlockSpec(memory_space=pl.ANY)
        bf, f32 = jnp.bfloat16, jnp.float32
        dma = pltpu.SemaphoreType.DMA
        n_dn = d_model // DOWN
        out = pl.pallas_call(
            functools.partial(kernel, (group, slots)),
            out_shape=jax.ShapeDtypeStruct((tokens, d_model), bf),
            in_specs=[smem] + [vmem] * 5 + [hbm] * 9,
            out_specs=vmem,
            scratch_shapes=[
                pltpu.VMEM((both, d_model), bf), pltpu.VMEM((both, d_model), bf), pltpu.VMEM((both, width), bf),
                pltpu.VMEM((both, ff), bf),
                pltpu.VMEM((layers, chips, 4, hd, rows), bf), pltpu.VMEM((layers, chips + 1, 4, hd + 8, rows), f32),
                pltpu.VMEM((2, pages, page, hd), bf), pltpu.VMEM((2, pages, hd, page), bf),
                pltpu.VMEM((2, tokens, hd), bf), pltpu.VMEM((2, hd, tokens), bf),
                pltpu.VMEM((2 * slots, page, rows), f32),
                pltpu.VMEM((2, both, d_model), f32), pltpu.VMEM((2, both, d_model), f32),
                pltpu.VMEM((d_model, width), bf), pltpu.VMEM((2, d_model, hd), bf),
                pltpu.VMEM((PAIRS, 2, d_model, CHUNK), bf), pltpu.VMEM((DOWNS, ff, DOWN), bf),
                dma((layers, chips, 4)), dma((layers, chips, 4)), dma((layers, chips, 4)), dma((layers, chips + 1, 4)),
                dma((layers, 2)), dma((layers, 2)), dma((layers, 2)), dma, dma,
                dma((layers, 2, n_dn)), dma((layers, 2, n_dn)),
                dma((3,)), dma((2,)), dma((PAIRS, 2)), dma((DOWNS,)),
            ],
            compiler_params=pltpu.CompilerParams(collective_id=0, has_side_effects=True, vmem_limit_bytes=67000000),
        )(table, x_loc[0], cos_t, sin_t, gains(norm_attn), gains(norm_mlp), k_pages, v_pages, wq, wk, wv, wo, w_gate, w_up, w_down)
        return out[None]

    return jax.shard_map(per_device, mesh=mesh, in_specs=(by_owner, by_owner, by_request, by_request, shared, shared, shared, shared, shared, shared, shared, shared, shared), out_specs=by_request, check_vma=False)
```

time: 990 us -> 271 us (0.27)
  waiting for transfers between devices: 549 us -> 0 us
  matrix products: 230 us -> 0 us
  Pallas kernels: 0 us -> 203 us
  local copies, waits for them, and re-layouts: 124 us -> 50.1 us
  other arithmetic: 63.6 us -> 0.42 us
  starting transfers between devices: 18.2 us -> 0 us
  blocking collectives: 0 us -> 16.3 us
    all_to_all x2 -> x0, waiting for transfers between devices: 549 us -> none  [per_device(): incoming = lax.all_to_all(outgoing, 'pool', 0, 0, tiled=True)]
    dot_general x22 -> x0, matrix products: 230 us -> none  [the longest x2 53.3 us: decoder_layer(): jnp.einsum('grtoks,oksgd->tgrd', prob_pre, v_pre, preferred_element_type=...]
    pallas_call x0 -> x1, Pallas kernels: none -> 203 us  [per_device(): pl.pallas_call(functools.partial(kernel, (group, slots)), out_shape=jax.S...]
    reduce_sum x5 -> x0, other arithmetic: 43.2 us -> none  [the longest x2 42.8 us: decoder_layer(): jnp.sum(exp_pre, axis=(3, 4, 5)) + jnp.sum(exp_new, axis=3)]
    dot_general x6 -> x0, local copies, waits for them, and re-layouts: 40.2 us -> none  [the longest x3 36.5 us: decoder_layer(): jnp.dot(h_attn, wq_l, preferred_element_type=jnp.float32)]
    unnamed x29 -> x16, local copies, waits for them, and re-layouts: 0.82 us -> 32.3 us
    gather x2 -> x0, local copies, waits for them, and re-layouts: 21.9 us -> none  [per_device(): jnp.take(pool_loc[layer], send_rows, axis=0)]
    reshape x5 -> x1, local copies, waits for them, and re-layouts: 21 us -> 0.09 us  [per_device(): idx_loc.reshape(-1)]
  transfers between devices with their start and end apart: 2 -> 0, of which waited for: 2 -> 0; matrix products, arithmetic and copies ran while one was open for 21% -> 0% of each run, Pallas kernels for 0% -> 0%
where the time goes in v1:
time: 271 us
  Pallas kernels  203 us (75%)
  local copies, waits for them, and re-layouts  50.1 us (18%)
  blocking collectives  16.3 us (6%)
    pallas_call x1, Pallas kernels, per_device(): pl.pallas_call(functools.partial(kernel, (group, slots)), out_shape=jax.S...  203 us
    unnamed x16, local copies, waits for them, and re-layouts  32.3 us
    unnamed x1, blocking collectives  16.3 us
    slice x1, local copies, waits for them, and re-layouts, per_device(): v_pages = jnp.transpose(pool_loc[:, :, 1], (0, 3, 1, 4, 2))  14.4 us

profile of v1, /device:TPU:21, one launch (start us, length us, event | category | flops | bytes accessed | tf_op | source)
XLA Modules:
  0.0 270.8 jit_solution(10000843927682010206)
XLA Ops:
  0.0 0.1 fusion.2
  0.2 0.1 pad_maximum_fusion
  0.2 0.6 tile.20
  0.9 0.8 tile.9.cos_ref
  1.7 14.4 %fusion.3 = (bf16[2,32,1,256,2,128]{5,4,3,2,1,0:T(2,128)(2,1)}, bf16[2,32,1,256,2,128]{5,4,3,2,1,0:T(2,128)(2,1)}) fusion(bf16[2,32,2,256,2,128]{5,4,3,2,1,0:T(2,128)(2,1)} %param.13), kind=kLoop, calls=%fused_computation.8 | loop fusion | bytes 33554432 | tf_op jit(solution)/shard_map/slice | solution.py:349
  16.0 8.8 %copy.23 = bf16[2,32,1,256,2,128]{5,3,1,4,0,2:T(8,128)(2,1)} copy(bf16[2,32,1,256,2,128]{5,4,3,2,1,0:T(2,128)(2,1)} %get-tuple-element.6) | data formatting | bytes 16777216
  24.9 0.0 copy-start.2
  24.9 0.0 copy-start.4
  24.9 0.0 copy-start.3
  24.9 0.0 copy-start
  24.9 0.0 copy-start.1
  24.9 21.1 %copy.21 = bf16[2,32,1,256,2,128]{3,5,1,4,0,2:T(8,128)(2,1)} copy(bf16[2,32,1,256,2,128]{5,4,3,2,1,0:T(2,128)(2,1)} %get-tuple-element.5) | data formatting | bytes 16777216
  46.0 0.0 copy-done.2
  46.0 0.1 copy.17
  46.1 0.1 reshape.37
  46.2 0.0 copy-done.4
  46.2 0.6 dynamic-slice
  47.4 0.0 copy-done.3
  47.4 0.2 add_dynamic-update-slice_fusion
  47.6 16.3 %all-reduce = s32[1280]{0:T(1024)S(1)} all-reduce(s32[1280]{0:T(1024)S(1)} %add_dynamic-update-slice_fusion), channel_id=2, replica_groups=mesh['replica'=4,'pool'=16] {'pool'}, use_global_device_ids=true, to_apply=%add | all-reduce | flops 1280 | bytes 10240
  63.9 0.7 reshape.41.tab
  64.6 0.0 copy-done
  64.6 0.6 reshape.39.ga_ref
  65.2 0.0 copy-done.1
  65.2 0.6 reshape.40.gm_ref
  65.8 203.3 %shard_map.127 = bf16[64,2048]{1,0:T(8,128)(2,1)} custom-call(s32[16,80]{1,0:T(8,128)} %reshape.41.tab, bf16[64,2048]{1,0:T(8,128)(2,1)} %bitcast.18, f32[128,128]{1,0:T(8,128)} %tile.9.cos_ref, f32[128,128]{1,0:T(8,128)} %bitcast.19, f32[2,1,2048]{2,1,0:T(1,128)} %reshape.39.ga_ref, f32[2,1,2048]{2,1,0:T(1,128)} %reshape.40.gm_ref, ...), custom_call_target="tpu_custom_call" | custom-call | tf_op jit(solution)/shard_map/pallas_call | solution.py:365
  269.1 1.7 copy.26
  (3 shorter events, 0.0 us)
Async XLA Ops:
  24.9 21.1 %copy-start.2 = (s32[16,1,4]{0,2,1:T(4,128)S(1)}, s32[16,1,4]{0,2,1:T(4,128)}, u32[]{:S(2)}) copy-start(s32[16,1,4]{0,2,1:T(4,128)} %param.14) | copy-start | bytes 772
  24.9 21.3 %copy-start.4 = (u32[64]{0:T(128)S(1)}, u32[64]{0:T(128)}, u32[]{:S(2)}) copy-start(u32[64]{0:T(128)} %constant.11) | copy-start | bytes 772
  24.9 22.5 %copy-start.3 = (s32[1,16]{1,0:T(1,128)S(1)}, s32[1,16]{1,0:T(1,128)}, u32[]{:S(2)}) copy-start(s32[1,16]{1,0:T(1,128)} %param.15) | copy-start | bytes 196
  24.9 39.7 %copy-start = (bf16[2,2048]{1,0:T(2,128)(2,1)S(1)}, bf16[2,2048]{1,0:T(2,128)(2,1)}, u32[]{:S(2)}) copy-start(bf16[2,2048]{1,0:T(2,128)(2,1)} %param.17) | copy-start | bytes 24580
  24.9 40.3 %copy-start.1 = (bf16[2,2048]{1,0:T(2,128)(2,1)S(1)}, bf16[2,2048]{1,0:T(2,128)(2,1)}, u32[]{:S(2)}) copy-start(bf16[2,2048]{1,0:T(2,128)(2,1)} %param.22) | copy-start | bytes 24580

commit v2 on v1

--- a/solution.py
+++ b/solution.py
@@ -15,6 +15,7 @@
 DOWN = 256
 PAIRS = 3
 DOWNS = 3
+LANDS = 4
 
 
 def rms_norm(vals_f, gain):
@@ -22,20 +23,25 @@
     return (vals_f * inv_rms * gain).astype(jnp.bfloat16)
 
 
+def when(cond):
+    return lambda body: body() if cond else None
+
+
 def dot32(a, b):
     return jnp.dot(a, b, preferred_element_type=jnp.float32)
 
 
-def kernel(dims, tab, x_ref, cos_ref, sin_ref, ga_ref, gm_ref, kp, vp, wq, wk, wv, wo, wg, wu, wd, out_ref,
-           xs, hs, avec, us, qbuf, acc, kpg, vpg, knew, vnew, scores, sent, got, wqo, wkv, gu, dn,
-           q_ss, q_rs, a_ss, a_rs, pg_ls, pg_ss, pg_rs, x_ss, x_rs, p_ss, p_rs, wq_s, wkv_s, gu_s, dn_s):
+def kernel(dims, meta_ref, x_ref, cos_ref, sin_ref, ga_ref, gm_ref, raw, wq, wk, wv, wo, wg, wu, wd, out_ref,
+           xs, hs, avec, us, qbuf, acc, aout, kpgs, vpgs, knew, vnew, scores, sent, got, wqo, wkv, gu, dn,
+           metas, tab, land, wide, stage_k, stage_v,
+           q_ss, q_rs, a_ss, a_rs, pg_ls, pg_ss, pg_rs, x_ss, x_rs, p_ss, p_rs, wq_s, wkv_s, gu_s, dn_s, m_ss, m_rs, t_s):
     group, slots = dims
     chips = group // 2
     layers, _, d_model = ga_ref.shape
     tokens = x_ref.shape[0]
-    hd = kp.shape[-1]
-    page = kp.shape[3]
-    pages = kp.shape[2]
+    hd = raw.shape[-1]
+    page = raw.shape[3] // 2
+    pages = raw.shape[1]
     width = wq.shape[2] // 2
     heads = width // hd
     part = tokens // 2
@@ -44,6 +50,7 @@
     n_gu = -(-ff // CHUNK)
     n_dn = d_model // DOWN
     n_out = d_model // CHUNK
+    share = -(-pages // (chips - 1))
     scale = hd ** -0.5 * LOG2E
 
     me = lax.axis_index("pool")
@@ -60,22 +67,65 @@
 
     def q_hop(layer, s, b):
         return pltpu.make_async_remote_copy(
-            src_ref=qbuf.at[layer, s, b], dst_ref=qbuf.at[layer, s + 1, b], send_sem=q_ss.at[layer, s, b], recv_sem=q_rs.at[layer, s + 1, b],
+            src_ref=qbuf.at[s, b], dst_ref=qbuf.at[s + 1, b], send_sem=q_ss.at[layer, s, b], recv_sem=q_rs.at[layer, s + 1, b],
             device_id=to(along(b)), device_id_type=pl.DeviceIdType.MESH)
 
     def a_hop(layer, s, b):
         return pltpu.make_async_remote_copy(
-            src_ref=acc.at[layer, s, b], dst_ref=acc.at[layer, s + 1, b], send_sem=a_ss.at[layer, s, b], recv_sem=a_rs.at[layer, s + 1, b],
+            src_ref=aout.at[lax.rem(s, 2), b], dst_ref=acc.at[s + 1, b], send_sem=a_ss.at[layer, s, b], recv_sem=a_rs.at[layer, s + 1, b],
             device_id=to(along(b)), device_id_type=pl.DeviceIdType.MESH)
 
-    def page_local(layer, which):
-        src, dst = (kp, kpg) if which == 0 else (vp, vpg)
-        return pltpu.make_async_copy(src.at[layer, c], dst.at[c], pg_ls.at[layer, which])
-
-    def page_remote(layer, which):
-        src, dst = (kp, kpg) if which == 0 else (vp, vpg)
+    def page_in(layer, pg):
+        slot = lax.rem(pg, LANDS)
+        return pltpu.make_async_copy(raw.at[layer, pg], land.at[slot], pg_ls.at[slot])
+
+    def page_out(layer, pg):
+        slot = lax.rem(pg, LANDS)
+        return [pltpu.make_async_remote_copy(
+            src_ref=src.at[slot], dst_ref=dst.at[c, pg], send_sem=pg_ss.at[slot, i], recv_sem=pg_rs.at[layer, i],
+            device_id=to(mate), device_id_type=pl.DeviceIdType.MESH) for i, (src, dst) in enumerate(((stage_k, kpgs[layer]), (stage_v, vpgs[layer])))]
+
+    def page_arrival(layer):
+        return [pltpu.make_async_remote_copy(
+            src_ref=dst.at[c], dst_ref=dst.at[1 - c], send_sem=pg_ss.at[0, i], recv_sem=pg_rs.at[layer, i],
+            device_id=to(mate), device_id_type=pl.DeviceIdType.MESH) for i, dst in enumerate((kpgs[layer], vpgs[layer]))]
+
+    def prepare(layer, pg):
+        slot = lax.rem(pg, LANDS)
+        page_in(layer, pg).wait()
+
+        @pl.when(pg >= LANDS)
+        def _():
+            for one in page_out(layer, pg):
+                one.wait_send()
+
+        for kind in range(2):
+            wide[kind] = land[slot, kind].astype(jnp.float32)
+        mine = pl.ds(c, page, stride=2)
+        other = pl.ds(1 - c, page, stride=2)
+        kpgs[layer][c, pg] = wide[0, mine, :].astype(jnp.bfloat16)
+        stage_k[slot] = wide[0, other, :].astype(jnp.bfloat16)
+        vpgs[layer][c, pg] = wide[1, mine, :].T.astype(jnp.bfloat16)
+        stage_v[slot] = wide[1, other, :].T.astype(jnp.bfloat16)
+        go(page_out(layer, pg))
+
+        @pl.when(pg + LANDS < pages)
+        def _():
+            page_in(layer, pg + LANDS).start()
+
+    def prepare_end(layer):
+        for pg in range(pages - LANDS, pages):
+            for one in page_out(layer, pg):
+                one.wait_send()
+
+    def meta_hop(off):
         return pltpu.make_async_remote_copy(
-            src_ref=src.at[layer, 1 - c], dst_ref=dst.at[c], send_sem=pg_ss.at[layer, which], recv_sem=pg_rs.at[layer, which],
+            src_ref=meta_ref, dst_ref=metas.at[me], send_sem=m_ss.at[off], recv_sem=m_rs.at[me],
+            device_id=to(lax.rem(me + off, group)), device_id_type=pl.DeviceIdType.MESH)
+
+    def meta_arrival(peer):
+        return pltpu.make_async_remote_copy(
+            src_ref=meta_ref, dst_ref=metas.at[peer], send_sem=m_ss.at[0], recv_sem=m_rs.at[peer],
             device_id=to(mate), device_id_type=pl.DeviceIdType.MESH)
 
     def part_hop(layer, k, n, size):
@@ -117,30 +167,48 @@
             one.wait()
 
     barrier = pltpu.get_barrier_semaphore()
-    for dev in (mate, along(0), along(2)):
-        pl.semaphore_signal(barrier, inc=1, device_id=to(dev), device_id_type=pl.DeviceIdType.MESH)
+    for off in range(1, group):
+        pl.semaphore_signal(barrier, inc=1, device_id=to(lax.rem(me + off, group)), device_id_type=pl.DeviceIdType.MESH)
+    for pg in range(LANDS):
+        page_in(0, pg).start()
     go(load_wq(0) + load_wkv(0))
-    go([page_local(0, 0), page_local(0, 1)])
-    pl.semaphore_wait(barrier, 3)
+    pl.semaphore_wait(barrier, group - 1)
 
     own = pl.ds(pl.multiple_of(c * tokens, tokens), tokens)
     x_swap = pltpu.make_async_remote_copy(
         src_ref=x_ref, dst_ref=xs.at[own], send_sem=x_ss, recv_sem=x_rs, device_id=to(mate), device_id_type=pl.DeviceIdType.MESH)
     x_swap.start()
-    go([page_remote(0, 0), page_remote(0, 1)])
+    for off in range(1, group):
+        meta_hop(off).start()
+    metas[me] = meta_ref[...]
     xs[own, :] = x_ref[...]
+
+    def first(pg, carry):
+        prepare(0, pg)
+        return carry
+
+    lax.fori_loop(0, pages, first, 0)
+    prepare_end(0)
     for i in range(PAIRS):
         go(load_gu(0, i, i))
     for i in range(DOWNS):
         go(load_dn(0, i, i))
+    for off in range(1, group):
+        meta_hop(off).wait_send()
+        meta_arrival(lax.rem(me + off, group)).wait_recv()
+    to_tab = pltpu.make_async_copy(metas.at[:, 0, :], tab, t_s)
+    to_tab.start()
+    to_tab.wait()
     x_swap.wait()
-
-    def attend(q_t, req, extra):
+    for pg in range(LANDS):
+        page_in(1, pg).start()
+
+    def attend(layer, q_t, req, extra):
         spots = [(o, j) for o in range(2) for j in range(slots)]
         valid, peaks = [], []
         for n, (o, j) in enumerate(spots):
             owner = 2 * z + o
-            s = dot32(kpg[o, tab[owner, req * slots + j]], q_t)
+            s = dot32(kpgs[layer][o, tab[owner, req * slots + j]], q_t)
             scores[n] = s
             ok = j < tab[req, group * slots + owner]
             valid.append(ok)
@@ -156,23 +224,25 @@
             shift = jnp.where(valid[n], -top, NEG)
             p = jnp.exp2(scores[n] * scale + shift)
             total = total + jnp.sum(p, axis=0, keepdims=True)
-            out = out + dot32(vpg[o, tab[owner, req * slots + j]], p.astype(jnp.bfloat16))
+            out = out + dot32(vpgs[layer][o, tab[owner, req * slots + j]], p.astype(jnp.bfloat16))
         if extra is not None:
             p = jnp.exp2(new_s * scale - top)
             total = total + jnp.sum(p, axis=0, keepdims=True)
             out = out + dot32(extra[1], p.astype(jnp.bfloat16))
         return out, top, total
 
-    def put_acc(layer, s, b, out, top, total):
-        acc[layer, s, b, :hd, :] = out
+    def put(ref, out, top, total):
+        ref[:hd, :] = out
         line = lax.broadcasted_iota(jnp.int32, (8, rows), 0)
-        acc[layer, s, b, hd:hd + 8, :] = jnp.where(line == 0, top, total)
-
-    def merge(layer, s, b, out, top, total):
-        in_out, in_top, in_total = acc[layer, s, b, :hd, :], acc[layer, s, b, hd:hd + 1, :], acc[layer, s, b, hd + 1:hd + 2, :]
-        best = jnp.maximum(top, in_top)
-        fa, fb = jnp.exp2(in_top - best), jnp.exp2(top - best)
-        return in_out * fa + out * fb, best, in_total * fa + total * fb
+        ref[hd:hd + 8, :] = jnp.where(line == 0, top, total)
+
+    def take(ref):
+        return ref[:hd, :], ref[hd:hd + 1, :], ref[hd + 1:hd + 2, :]
+
+    def merge(one, two):
+        best = jnp.maximum(one[1], two[1])
+        fa, fb = jnp.exp2(one[1] - best), jnp.exp2(two[1] - best)
+        return one[0] * fa + two[0] * fb, best, one[2] * fa + two[2] * fb
 
     def rope(vals):
         return vals * cos_ref[...] + pltpu.roll(vals, hd // 2, axis=1) * sin_ref[...]
@@ -193,28 +263,27 @@
         for b in range(4):
             lo = (b % 2) * tokens + (b // 2) * part
             q_rows = jnp.concatenate([avec[lo:lo + part, n * hd:(n + 1) * hd] for n in range(heads)], axis=0)
-            qbuf[layer, 0, b] = q_rows.astype(jnp.float32).T.astype(jnp.bfloat16)
+            qbuf[0, b] = q_rows.astype(jnp.float32).T.astype(jnp.bfloat16)
             q_hop(layer, 0, b).start()
         go(load_wo(layer))
 
-        @pl.when(layer + 1 < layers)
+        @when(layer + 1 < layers)
         def _():
             go(load_wkv(layer + 1))
 
         for b in range(4):
-            put_acc(layer, 1, b, jnp.zeros((hd, rows), jnp.float32), jnp.full((1, rows), NEG), jnp.zeros((1, rows), jnp.float32))
-        for which in range(2):
-            page_local(layer, which).wait()
-            page_remote(layer, which).wait()
+            put(acc.at[1, b], jnp.zeros((hd, rows), jnp.float32), jnp.full((1, rows), NEG), jnp.zeros((1, rows), jnp.float32))
+        for one in page_arrival(layer):
+            one.wait_recv()
 
         def home(b, carry):
             i = lax.rem(b, 2)
-            q_t = qbuf[layer, 0, b]
+            q_t = qbuf[0, b]
             s = dot32(knew[i], q_t)
             key = lax.broadcasted_iota(jnp.int32, s.shape, 0)
             tok = lax.rem(lax.broadcasted_iota(jnp.int32, s.shape, 1), part) + (b // 2) * part
             s = jnp.where(key <= tok, s, NEG)
-            put_acc(layer, 0, b, *attend(q_t, 2 * z + i, (s, vnew[i])))
+            put(acc.at[0, b], *attend(layer, q_t, 2 * z + i, (s, vnew[i])))
             return carry
 
         lax.fori_loop(0, 4, home, 0)
@@ -229,35 +298,54 @@
 
             def block(b, carry):
                 source = lax.rem(z + jnp.where(b < 2, chips - s, s), chips)
-                found = attend(qbuf[layer, s, b], 2 * source + lax.rem(b, 2), None)
+                found = attend(layer, qbuf[s, b], 2 * source + lax.rem(b, 2), None)
 
                 @pl.when(s >= 2)
                 def _():
                     a_hop(layer, s - 1, b).wait_recv()
 
-                put_acc(layer, s, b, *merge(layer, s, b, *found))
+                @pl.when(s >= 3)
+                def _():
+                    a_hop(layer, s - 2, b).wait_send()
+
+                @pl.when(s < chips - 1)
+                def _():
+                    q_hop(layer, s, b).wait_send()
+
+                put(aout.at[lax.rem(s, 2), b], *merge(take(acc.at[s, b]), found))
                 a_hop(layer, s, b).start()
                 return carry
 
-            return lax.fori_loop(0, 4, block, carry)
+            lax.fori_loop(0, 4, block, 0)
+
+            @when(layer + 1 < layers)
+            def _():
+                def one_page(n, carry):
+                    prepare(layer + 1, n)
+                    return carry
+
+                lax.fori_loop((s - 1) * share, jnp.minimum(s * share, pages), one_page, 0)
+
+            return carry
 
         lax.fori_loop(1, chips, step, 0)
+
+        @when(layer + 1 < layers)
+        def _():
+            prepare_end(layer + 1)
 
         for b in range(4):
             a_hop(layer, chips - 1, b).wait_recv()
-            out, top, total = merge(layer, chips, b, acc[layer, 0, b, :hd, :], acc[layer, 0, b, hd:hd + 1, :], acc[layer, 0, b, hd + 1:hd + 2, :])
+            out, top, total = merge(take(acc.at[chips, b]), take(acc.at[0, b]))
             a_rows = (out / total).T.astype(jnp.bfloat16)
             lo = (b % 2) * tokens + (b // 2) * part
             for n in range(heads):
                 avec[lo:lo + part, n * hd:(n + 1) * hd] = a_rows[n * part:(n + 1) * part]
 
-        def drain(s, carry):
-            for b in range(4):
-                q_hop(layer, s, b).wait_send()
-                a_hop(layer, s + 1, b).wait_send()
-            return carry
-
-        lax.fori_loop(0, chips - 1, drain, 0)
+        for b in range(4):
+            q_hop(layer, 0, b).wait_send()
+            a_hop(layer, chips - 2, b).wait_send()
+            a_hop(layer, chips - 1, b).wait_send()
 
         done(load_wo(layer))
         for n in range(n_out):
@@ -265,7 +353,7 @@
             sent[0, :, n * CHUNK:(n + 1) * CHUNK] = dot32(avec[...], wqo[half * width:(half + 1) * width, off:off + CHUNK])
             part_hop(layer, 0, n, CHUNK).start()
 
-        @pl.when(layer + 1 < layers)
+        @when(layer + 1 < layers)
         def _():
             go(load_wq(layer + 1))
 
@@ -273,10 +361,6 @@
             part_hop(layer, 0, n, CHUNK).wait()
         x_mid = (xs[...].astype(jnp.float32) + (sent[0] + got[0])).astype(jnp.bfloat16)
         xs[...] = x_mid
-
-        @pl.when(layer + 1 < layers)
-        def _():
-            go([page_local(layer + 1, 0), page_local(layer + 1, 1), page_remote(layer + 1, 0), page_remote(layer + 1, 1)])
 
         hs[...] = rms_norm(xs[...].astype(jnp.float32), gm_ref[layer])
 
@@ -294,7 +378,7 @@
 
             @pl.when(jnp.logical_and(ahead >= n_gu, layer + 1 < layers))
             def _():
-                go(load_gu(layer + 1, ahead - n_gu, slot))
+                go(load_gu(min(layer + 1, layers - 1), ahead - n_gu, slot))
 
             return carry
 
@@ -313,7 +397,7 @@
 
             @pl.when(jnp.logical_and(ahead >= n_dn, layer + 1 < layers))
             def _():
-                go(load_dn(layer + 1, ahead - n_dn, slot))
+                go(load_dn(min(layer + 1, layers - 1), ahead - n_dn, slot))
 
             return carry
 
@@ -323,7 +407,8 @@
         xs[...] = (xs[...].astype(jnp.float32) + (sent[1] + got[1])).astype(jnp.bfloat16)
         return carry
 
-    lax.fori_loop(0, layers, layer_body, 0)
+    for layer in range(layers):
+        layer_body(layer, 0)
     out_ref[...] = xs[own, :]
 
 
@@ -344,9 +429,9 @@
         ff = w_gate.shape[2] // 2
         both = 2 * tokens
 
-        table = lax.all_gather(jnp.concatenate([idx_loc.reshape(-1), count_loc.reshape(-1)]), "pool")
-        k_pages = jnp.transpose(pool_loc[:, :, 0], (0, 3, 1, 2, 4))
-        v_pages = jnp.transpose(pool_loc[:, :, 1], (0, 3, 1, 4, 2))
+        meta = jnp.concatenate([idx_loc.reshape(-1), count_loc.reshape(-1)])
+        meta = jnp.broadcast_to(jnp.pad(meta, (0, 128 - meta.shape[0])), (8, 128))
+        raw = pool_loc.reshape(layers, pages, 2, page * kv_heads, hd)
         half = hd // 2
         freqs = ROPE_BASE ** (-jnp.arange(half, dtype=jnp.float32) / half)
         angles = jnp.arange(tokens, dtype=jnp.float32)[:, None] * freqs[None, :]
@@ -357,7 +442,6 @@
             return one.astype(jnp.float32)[:, None]
 
         vmem = pl.BlockSpec(memory_space=pltpu.VMEM)
-        smem = pl.BlockSpec(memory_space=pltpu.SMEM)
         hbm = pl.BlockSpec(memory_space=pl.ANY)
         bf, f32 = jnp.bfloat16, jnp.float32
         dma = pltpu.SemaphoreType.DMA
@@ -365,25 +449,29 @@
         out = pl.pallas_call(
             functools.partial(kernel, (group, slots)),
             out_shape=jax.ShapeDtypeStruct((tokens, d_model), bf),
-            in_specs=[smem] + [vmem] * 5 + [hbm] * 9,
+            in_specs=[vmem] * 6 + [hbm] * 8,
             out_specs=vmem,
             scratch_shapes=[
                 pltpu.VMEM((both, d_model), bf), pltpu.VMEM((both, d_model), bf), pltpu.VMEM((both, width), bf),
                 pltpu.VMEM((both, ff), bf),
-                pltpu.VMEM((layers, chips, 4, hd, rows), bf), pltpu.VMEM((layers, chips + 1, 4, hd + 8, rows), f32),
-                pltpu.VMEM((2, pages, page, hd), bf), pltpu.VMEM((2, pages, hd, page), bf),
+                pltpu.VMEM((chips, 4, hd, rows), bf), pltpu.VMEM((chips + 1, 4, hd + 8, rows), f32), pltpu.VMEM((2, 4, hd + 8, rows), f32),
+                [pltpu.VMEM((2, pages, page, hd), bf)] * layers, [pltpu.VMEM((2, pages, hd, page), bf)] * layers,
                 pltpu.VMEM((2, tokens, hd), bf), pltpu.VMEM((2, hd, tokens), bf),
                 pltpu.VMEM((2 * slots, page, rows), f32),
                 pltpu.VMEM((2, both, d_model), f32), pltpu.VMEM((2, both, d_model), f32),
                 pltpu.VMEM((d_model, width), bf), pltpu.VMEM((2, d_model, hd), bf),
                 pltpu.VMEM((PAIRS, 2, d_model, CHUNK), bf), pltpu.VMEM((DOWNS, ff, DOWN), bf),
+                pltpu.VMEM((group, 8, 128), jnp.int32), pltpu.SMEM((group, 128), jnp.int32),
+                pltpu.VMEM((LANDS, 2, 2 * page, hd), bf), pltpu.VMEM((2, 2 * page, hd), f32),
+                pltpu.VMEM((LANDS, page, hd), bf), pltpu.VMEM((LANDS, hd, page), bf),
                 dma((layers, chips, 4)), dma((layers, chips, 4)), dma((layers, chips, 4)), dma((layers, chips + 1, 4)),
-                dma((layers, 2)), dma((layers, 2)), dma((layers, 2)), dma, dma,
+                dma((LANDS,)), dma((LANDS, 2)), dma((layers, 2)), dma, dma,
                 dma((layers, 2, n_dn)), dma((layers, 2, n_dn)),
                 dma((3,)), dma((2,)), dma((PAIRS, 2)), dma((DOWNS,)),
+                dma((group,)), dma((group,)), dma,
             ],
             compiler_params=pltpu.CompilerParams(collective_id=0, has_side_effects=True, vmem_limit_bytes=67000000),
-        )(table, x_loc[0], cos_t, sin_t, gains(norm_attn), gains(norm_mlp), k_pages, v_pages, wq, wk, wv, wo, w_gate, w_up, w_down)
+        )(meta, x_loc[0], cos_t, sin_t, gains(norm_attn), gains(norm_mlp), raw, wq, wk, wv, wo, w_gate, w_up, w_down)
         return out[None]
 
     return jax.shard_map(per_device, mesh=mesh, in_specs=(by_owner, by_owner, by_request, by_request, shared, shared, shared, shared, shared, shared, shared, shared, shared), out_specs=by_request, check_vma=False)

time: 271 us -> 223 us (0.82)
  local copies, waits for them, and re-layouts: 50.1 us -> 7.16 us
  blocking collectives: 16.3 us -> 0 us
  Pallas kernels: 203 us -> 214 us
    unnamed x16 -> x2, local copies, waits for them, and re-layouts: 32.3 us -> 2.43 us
    unnamed x1 -> x0, blocking collectives: 16.3 us -> none
    slice x1 -> x0, local copies, waits for them, and re-layouts: 14.4 us -> none  [per_device(): v_pages = jnp.transpose(pool_loc[:, :, 1], (0, 3, 1, 4, 2))]
    pallas_call x1, Pallas kernels: 203 us -> 214 us  [per_device(): pl.pallas_call(functools.partial(kernel, (group, slots)), out_shape=jax.S...]
where the time goes in v2:
time: 223 us; the launch traced here: 222 us
  Pallas kernels  214 us (96%)
  local copies, waits for them, and re-layouts  7.16 us (3%)
    pallas_call x1, Pallas kernels, per_device(): pl.pallas_call(functools.partial(kernel, (group, slots)), out_shape=jax.S...  214 us

profile of v2, /device:TPU:21, one launch (start us, length us, event | category | flops | bytes accessed | tf_op | source)
XLA Modules:
  0.0 222.4 jit_solution(365832672751167697)
XLA Ops:
  0.0 0.8 copy.15
  0.8 0.1 reshape.40
  0.9 0.7 pad_add_fusion
  1.6 0.6 broadcast_in_dim.18.meta_ref
  2.2 1.3 reshape.43.ga_ref
  3.5 1.3 reshape.44.gm_ref
  4.8 0.1 fusion.2
  5.0 0.1 pad_maximum_fusion
  5.0 0.6 tile.20
  5.7 0.8 tile.9.cos_ref
  6.5 214.2 %shard_map.127 = bf16[64,2048]{1,0:T(8,128)(2,1)} custom-call(s32[8,128]{1,0:T(8,128)} %broadcast_in_dim.18.meta_ref, bf16[64,2048]{1,0:T(8,128)(2,1)} %bitcast.9, f32[128,128]{1,0:T(8,128)} %tile.9.cos_ref, f32[128,128]{1,0:T(8,128)} %bitcast.10, f32[2,1,2048]{2,1,0:T(1,128)} %reshape.43.ga_ref, f32[2,1,2048]{2,1,0:T(1,128)} %reshape.44.gm_ref, ...), custom_call_target="tpu_custom_call" | custom-call | tf_op jit(solution)/shard_map/pallas_call | solution.py:449
  220.7 1.7 copy.17
  (3 shorter events, 0.1 us)

commit v3 on v2

--- a/solution.py
+++ b/solution.py
@@ -32,7 +32,7 @@
 
 
 def kernel(dims, meta_ref, x_ref, cos_ref, sin_ref, ga_ref, gm_ref, raw, wq, wk, wv, wo, wg, wu, wd, out_ref,
-           xs, hs, avec, us, qbuf, acc, aout, kpgs, vpgs, knew, vnew, scores, sent, got, wqo, wkv, gu, dn,
+           xs, hs, avec, qtmp, us, qbuf, acc, aout, found, kpgs, vpgs, knew, vnew, scores, sent, got, wqo, wkv, gu, dn,
            metas, tab, land, wide, stage_k, stage_v,
            q_ss, q_rs, a_ss, a_rs, pg_ls, pg_ss, pg_rs, x_ss, x_rs, p_ss, p_rs, wq_s, wkv_s, gu_s, dn_s, m_ss, m_rs, t_s):
     group, slots = dims
@@ -52,6 +52,8 @@
     n_out = d_model // CHUNK
     share = -(-pages // (chips - 1))
     scale = hd ** -0.5 * LOG2E
+    rings = 2 * layers
+    lanes = rows // 2
 
     me = lax.axis_index("pool")
     z = me // 2
@@ -59,20 +61,21 @@
     mate = me + 1 - 2 * c
 
     def along(b):
-        delta = jnp.where(b < 2, 1, chips - 1)
+        delta = jnp.where(b < 1, 1, chips - 1)
         return lax.rem(z + delta, chips) * 2 + c
 
     def to(dev):
         return {"pool": dev}
 
-    def q_hop(layer, s, b):
+    def q_hop(k, s, b):
         return pltpu.make_async_remote_copy(
-            src_ref=qbuf.at[s, b], dst_ref=qbuf.at[s + 1, b], send_sem=q_ss.at[layer, s, b], recv_sem=q_rs.at[layer, s + 1, b],
+            src_ref=qbuf.at[k % 2, s, b], dst_ref=qbuf.at[k % 2, s + 1, b], send_sem=q_ss.at[k, s, b], recv_sem=q_rs.at[k, s + 1, b],
             device_id=to(along(b)), device_id_type=pl.DeviceIdType.MESH)
 
-    def a_hop(layer, s, b):
+    def a_hop(k, s, b, h):
         return pltpu.make_async_remote_copy(
-            src_ref=aout.at[lax.rem(s, 2), b], dst_ref=acc.at[s + 1, b], send_sem=a_ss.at[layer, s, b], recv_sem=a_rs.at[layer, s + 1, b],
+            src_ref=aout.at[k % 2, lax.rem(s, 2), b, h], dst_ref=acc.at[k % 2, s + 1, b, h],
+            send_sem=a_ss.at[k, s, b, h], recv_sem=a_rs.at[k, s + 1, b, h],
             device_id=to(along(b)), device_id_type=pl.DeviceIdType.MESH)
 
     def page_in(layer, pg):
@@ -128,10 +131,10 @@
             src_ref=meta_ref, dst_ref=metas.at[peer], send_sem=m_ss.at[0], recv_sem=m_rs.at[peer],
             device_id=to(mate), device_id_type=pl.DeviceIdType.MESH)
 
-    def part_hop(layer, k, n, size):
+    def part_hop(k, kind, n, size):
         cols = pl.ds(pl.multiple_of(n * size, size), size)
         return pltpu.make_async_remote_copy(
-            src_ref=sent.at[k, :, cols], dst_ref=got.at[k, :, cols], send_sem=p_ss.at[layer, k, n], recv_sem=p_rs.at[layer, k, n],
+            src_ref=sent.at[kind, :, cols], dst_ref=got.at[kind, :, cols], send_sem=p_ss.at[k, kind, n], recv_sem=p_rs.at[k, kind, n],
             device_id=to(mate), device_id_type=pl.DeviceIdType.MESH)
 
     def load_wq(layer):
@@ -200,9 +203,6 @@
     to_tab.start()
     to_tab.wait()
     x_swap.wait()
-    for pg in range(LANDS):
-        page_in(1, pg).start()
-
     def attend(layer, q_t, req, extra):
         spots = [(o, j) for o in range(2) for j in range(slots)]
         valid, peaks = [], []
@@ -232,9 +232,11 @@
         return out, top, total
 
     def put(ref, out, top, total):
-        ref[:hd, :] = out
         line = lax.broadcasted_iota(jnp.int32, (8, rows), 0)
-        ref[hd:hd + 8, :] = jnp.where(line == 0, top, total)
+        tail = jnp.where(line == 0, top, total)
+        for h in range(2):
+            ref[h, :hd, :] = out[:, h * lanes:(h + 1) * lanes]
+            ref[h, hd:hd + 8, :] = tail[:, h * lanes:(h + 1) * lanes]
 
     def take(ref):
         return ref[:hd, :], ref[hd:hd + 1, :], ref[hd + 1:hd + 2, :]
@@ -245,170 +247,237 @@
         return one[0] * fa + two[0] * fb, best, one[2] * fa + two[2] * fb
 
     def rope(vals):
-        return vals * cos_ref[...] + pltpu.roll(vals, hd // 2, axis=1) * sin_ref[...]
-
-    def layer_body(layer, carry):
-        last = layer == layers - 1
-        hs[...] = rms_norm(xs[...].astype(jnp.float32), ga_ref[layer])
-        done(load_wkv(layer))
-        k_all = rope(dot32(hs[...], wkv[0])).astype(jnp.bfloat16)
-        v_all = dot32(hs[...], wkv[1])
-        for i in range(2):
-            knew[i] = k_all[i * tokens:(i + 1) * tokens]
-            vnew[i] = v_all[i * tokens:(i + 1) * tokens].T.astype(jnp.bfloat16)
+        return vals * cos_ref[:vals.shape[0]] + pltpu.roll(vals, hd // 2, axis=1) * sin_ref[:vals.shape[0]]
+
+    def project(layer, streams):
+        first, count = streams[0] * tokens, len(streams) * tokens
+        hs[:count] = rms_norm(xs[first:first + count].astype(jnp.float32), ga_ref[layer])
+        h_all = hs[:count]
+        k_all = rope(dot32(h_all, wkv[0])).astype(jnp.bfloat16)
+        v_all = dot32(h_all, wkv[1])
+        for n, i in enumerate(streams):
+            knew[i] = k_all[n * tokens:(n + 1) * tokens]
+            vnew[i] = v_all[n * tokens:(n + 1) * tokens].T.astype(jnp.bfloat16)
         done(load_wq(layer))
         for n in range(heads):
-            q_head = rope(dot32(hs[...], wqo[:, n * hd:(n + 1) * hd])).astype(jnp.bfloat16)
-            avec[:, n * hd:(n + 1) * hd] = q_head
-        for b in range(4):
-            lo = (b % 2) * tokens + (b // 2) * part
-            q_rows = jnp.concatenate([avec[lo:lo + part, n * hd:(n + 1) * hd] for n in range(heads)], axis=0)
-            qbuf[0, b] = q_rows.astype(jnp.float32).T.astype(jnp.bfloat16)
-            q_hop(layer, 0, b).start()
-        go(load_wo(layer))
-
-        @when(layer + 1 < layers)
-        def _():
-            go(load_wkv(layer + 1))
-
-        for b in range(4):
-            put(acc.at[1, b], jnp.zeros((hd, rows), jnp.float32), jnp.full((1, rows), NEG), jnp.zeros((1, rows), jnp.float32))
-        for one in page_arrival(layer):
-            one.wait_recv()
-
-        def home(b, carry):
-            i = lax.rem(b, 2)
-            q_t = qbuf[0, b]
-            s = dot32(knew[i], q_t)
-            key = lax.broadcasted_iota(jnp.int32, s.shape, 0)
-            tok = lax.rem(lax.broadcasted_iota(jnp.int32, s.shape, 1), part) + (b // 2) * part
-            s = jnp.where(key <= tok, s, NEG)
-            put(acc.at[0, b], *attend(layer, q_t, 2 * z + i, (s, vnew[i])))
-            return carry
-
-        lax.fori_loop(0, 4, home, 0)
-
-        def step(s, carry):
-            for b in range(4):
-                q_hop(layer, s - 1, b).wait_recv()
-
-                @pl.when(s < chips - 1)
-                def _():
-                    q_hop(layer, s, b).start()
-
-            def block(b, carry):
-                source = lax.rem(z + jnp.where(b < 2, chips - s, s), chips)
-                found = attend(layer, qbuf[s, b], 2 * source + lax.rem(b, 2), None)
-
-                @pl.when(s >= 2)
-                def _():
-                    a_hop(layer, s - 1, b).wait_recv()
-
-                @pl.when(s >= 3)
-                def _():
-                    a_hop(layer, s - 2, b).wait_send()
-
-                @pl.when(s < chips - 1)
-                def _():
-                    q_hop(layer, s, b).wait_send()
-
-                put(aout.at[lax.rem(s, 2), b], *merge(take(acc.at[s, b]), found))
-                a_hop(layer, s, b).start()
-                return carry
-
-            lax.fori_loop(0, 4, block, 0)
-
-            @when(layer + 1 < layers)
-            def _():
-                def one_page(n, carry):
-                    prepare(layer + 1, n)
-                    return carry
-
-                lax.fori_loop((s - 1) * share, jnp.minimum(s * share, pages), one_page, 0)
-
-            return carry
-
-        lax.fori_loop(1, chips, step, 0)
-
-        @when(layer + 1 < layers)
-        def _():
-            prepare_end(layer + 1)
-
-        for b in range(4):
-            a_hop(layer, chips - 1, b).wait_recv()
-            out, top, total = merge(take(acc.at[chips, b]), take(acc.at[0, b]))
-            a_rows = (out / total).T.astype(jnp.bfloat16)
-            lo = (b % 2) * tokens + (b // 2) * part
-            for n in range(heads):
-                avec[lo:lo + part, n * hd:(n + 1) * hd] = a_rows[n * part:(n + 1) * part]
-
-        for b in range(4):
-            q_hop(layer, 0, b).wait_send()
-            a_hop(layer, chips - 2, b).wait_send()
-            a_hop(layer, chips - 1, b).wait_send()
-
-        done(load_wo(layer))
+            qtmp[:count, n * hd:(n + 1) * hd] = rope(dot32(h_all, wqo[:, n * hd:(n + 1) * hd])).astype(jnp.bfloat16)
+        for n, i in enumerate(streams):
+            for b in range(2):
+                lo = n * tokens + b * part
+                q_rows = jnp.concatenate([qtmp[lo:lo + part, m * hd:(m + 1) * hd] for m in range(heads)], axis=0)
+                qbuf[i, 0, b] = q_rows.astype(jnp.float32).T.astype(jnp.bfloat16)
+
+    def finish(k):
+        i = k % 2
+        for b in range(2):
+            for h in range(2):
+                a_hop(k, chips - 1, b, h).wait_recv()
+                out, top, total = merge(take(acc.at[i, chips, b, h]), take(acc.at[i, 0, b, h]))
+                a_rows = (out / total).T.astype(jnp.bfloat16)
+                for n in range(lanes // part):
+                    head = h * (lanes // part) + n
+                    avec[b * part:(b + 1) * part, head * hd:(head + 1) * hd] = a_rows[n * part:(n + 1) * part]
+        for b in range(2):
+            q_hop(k, 0, b).wait_send()
+            for h in range(2):
+                a_hop(k, chips - 2, b, h).wait_send()
+                a_hop(k, chips - 1, b, h).wait_send()
+        done(load_wo(k // 2))
         for n in range(n_out):
             half, off = divmod(n * CHUNK, width)
             sent[0, :, n * CHUNK:(n + 1) * CHUNK] = dot32(avec[...], wqo[half * width:(half + 1) * width, off:off + CHUNK])
-            part_hop(layer, 0, n, CHUNK).start()
-
-        @when(layer + 1 < layers)
-        def _():
-            go(load_wq(layer + 1))
-
+            part_hop(k, 0, n, CHUNK).start()
+        if k // 2 + 1 < layers:
+            go(load_wq(k // 2 + 1))
+        elif k + 1 < rings:
+            go(load_wo((k + 1) // 2))
+
+    def middle(k):
+        mine = slice((k % 2) * tokens, (k % 2 + 1) * tokens)
         for n in range(n_out):
-            part_hop(layer, 0, n, CHUNK).wait()
-        x_mid = (xs[...].astype(jnp.float32) + (sent[0] + got[0])).astype(jnp.bfloat16)
-        xs[...] = x_mid
-
-        hs[...] = rms_norm(xs[...].astype(jnp.float32), gm_ref[layer])
-
-        def gate_up(i, carry):
-            slot = lax.rem(layer * n_gu + i, PAIRS)
-            done(load_gu(layer, i, slot))
-            gate = dot32(hs[...], gu[slot, 0])
-            up = dot32(hs[...], gu[slot, 1])
+            part_hop(k, 0, n, CHUNK).wait()
+        xs[mine] = (xs[mine].astype(jnp.float32) + (sent[0] + got[0])).astype(jnp.bfloat16)
+        hs[:tokens] = rms_norm(xs[mine].astype(jnp.float32), gm_ref[k // 2])
+
+    def gate_up(k, lo, hi):
+        def body(i, carry):
+            slot = lax.rem(k * n_gu + i, PAIRS)
+            done(load_gu(k // 2, i, slot))
+            gate = dot32(hs[:tokens], gu[slot, 0])
+            up = dot32(hs[:tokens], gu[slot, 1])
             us[:, pl.ds(gu_start(i), CHUNK)] = (gate * (1.0 / (1.0 + jnp.exp(-gate))) * up).astype(jnp.bfloat16)
             ahead = i + PAIRS
 
             @pl.when(ahead < n_gu)
             def _():
-                go(load_gu(layer, ahead, slot))
-
-            @pl.when(jnp.logical_and(ahead >= n_gu, layer + 1 < layers))
-            def _():
-                go(load_gu(min(layer + 1, layers - 1), ahead - n_gu, slot))
+                go(load_gu(k // 2, ahead, slot))
+
+            if k + 1 < rings:
+                @pl.when(ahead >= n_gu)
+                def _():
+                    go(load_gu((k + 1) // 2, ahead - n_gu, slot))
 
             return carry
 
-        lax.fori_loop(0, n_gu, gate_up, 0)
-
-        def down(i, carry):
-            slot = lax.rem(layer * n_dn + i, DOWNS)
-            done(load_dn(layer, i, slot))
+        lax.fori_loop(lo, hi, body, 0)
+
+    def down(k, lo, hi):
+        def body(i, carry):
+            slot = lax.rem(k * n_dn + i, DOWNS)
+            done(load_dn(k // 2, i, slot))
             sent[1, :, pl.ds(pl.multiple_of(i * DOWN, DOWN), DOWN)] = dot32(us[...], dn[slot])
-            part_hop(layer, 1, i, DOWN).start()
+            part_hop(k, 1, i, DOWN).start()
             ahead = i + DOWNS
 
             @pl.when(ahead < n_dn)
             def _():
-                go(load_dn(layer, ahead, slot))
-
-            @pl.when(jnp.logical_and(ahead >= n_dn, layer + 1 < layers))
+                go(load_dn(k // 2, ahead, slot))
+
+            if k + 1 < rings:
+                @pl.when(ahead >= n_dn)
+                def _():
+                    go(load_dn((k + 1) // 2, ahead - n_dn, slot))
+
+            return carry
+
+        lax.fori_loop(lo, hi, body, 0)
+
+    def close(k):
+        mine = slice((k % 2) * tokens, (k % 2 + 1) * tokens)
+        for n in range(n_dn):
+            part_hop(k, 1, n, DOWN).wait()
+        xs[mine] = (xs[mine].astype(jnp.float32) + (sent[1] + got[1])).astype(jnp.bfloat16)
+        if k // 2 + 1 < layers:
+            if k % 2 == 0:
+                done(load_wkv(k // 2 + 1))
+            project(k // 2 + 1, (k % 2,))
+            go(load_wo((k + 1) // 2))
+            if k % 2 == 1 and k // 2 + 2 < layers:
+                go(load_wkv(k // 2 + 2))
+            for b in range(2):
+                q_hop(k + 2, 0, b).start()
+
+    def follow(k, s):
+        steps = chips - 1
+        up_steps = steps // 2
+        per_up = -(-n_gu // up_steps)
+        down_steps = steps - 2 - up_steps
+        per_down = -(-n_dn // down_steps)
+
+        @pl.when(s == 1)
+        def _():
+            finish(k)
+
+        @pl.when(s == 2)
+        def _():
+            middle(k)
+
+        up_lo = jnp.clip((s - 2) * per_up, 0, n_gu)
+        gate_up(k, up_lo, jnp.where(s >= 2, jnp.clip((s - 1) * per_up, 0, n_gu), up_lo))
+        at = s - 2 - up_steps
+        down_lo = jnp.clip(at * per_down, 0, n_dn)
+        down(k, down_lo, jnp.where(at >= 0, jnp.clip((at + 1) * per_down, 0, n_dn), down_lo))
+
+        @pl.when(s == steps)
+        def _():
+            close(k)
+
+    def ring(k):
+        layer, i = divmod(k, 2)
+        for b in range(2):
+            for h in range(2):
+                acc[i, 1, b, h, :, :] = jnp.where(lax.broadcasted_iota(jnp.int32, (hd + 8, lanes), 0) == hd, NEG, 0.0)
+        if i == 0:
+            for one in page_arrival(layer):
+                one.wait_recv()
+
+        def home(b, carry):
+            q_t = qbuf[i, 0, b]
+            s = dot32(knew[i], q_t)
+            key = lax.broadcasted_iota(jnp.int32, s.shape, 0)
+            tok = lax.rem(lax.broadcasted_iota(jnp.int32, s.shape, 1), part) + b * part
+            s = jnp.where(key <= tok, s, NEG)
+            put(acc.at[i, 0, b], *attend(layer, q_t, 2 * z + i, (s, vnew[i])))
+            return carry
+
+        lax.fori_loop(0, 2, home, 0)
+
+        def step(s, carry):
+            for b in range(2):
+                q_hop(k, s - 1, b).wait_recv()
+
+                @pl.when(s < chips - 1)
+                def _():
+                    q_hop(k, s, b).start()
+
+            def block(b, carry):
+                source = lax.rem(z + jnp.where(b < 1, chips - s, s), chips)
+                put(found.at[b], *attend(layer, qbuf[i, s, b], 2 * source + i, None))
+                return carry
+
+            lax.fori_loop(0, 2, block, 0)
+            if k > 0:
+                follow(k - 1, s)
+            else:
+                if layers > 1:
+                    def one_page(n, carry):
+                        prepare(1, n)
+                        return carry
+
+                    lax.fori_loop((s - 1) * share, jnp.minimum(s * share, pages), one_page, 0)
+
+                @pl.when(s == chips - 1)
+                def _():
+                    for b in range(2):
+                        q_hop(1, 0, b).start()
+
+            @pl.when(s < chips - 1)
             def _():
-                go(load_dn(min(layer + 1, layers - 1), ahead - n_dn, slot))
-
-            return carry
-
-        lax.fori_loop(0, n_dn, down, 0)
-        for n in range(n_dn):
-            part_hop(layer, 1, n, DOWN).wait()
-        xs[...] = (xs[...].astype(jnp.float32) + (sent[1] + got[1])).astype(jnp.bfloat16)
-        return carry
-
-    for layer in range(layers):
-        layer_body(layer, 0)
+                for b in range(2):
+                    q_hop(k, s, b).wait_send()
+
+            def pass_on(n, carry):
+                h, b = n // 2, lax.rem(n, 2)
+
+                @pl.when(s >= 2)
+                def _():
+                    a_hop(k, s - 1, b, h).wait_recv()
+
+                @pl.when(s >= 3)
+                def _():
+                    a_hop(k, s - 2, b, h).wait_send()
+
+                out, top, total = merge(take(acc.at[i, s, b, h]), take(found.at[b, h]))
+                slot = lax.rem(s, 2)
+                aout[i, slot, b, h, :hd, :] = out
+                line = lax.broadcasted_iota(jnp.int32, (8, lanes), 0)
+                aout[i, slot, b, h, hd:hd + 8, :] = jnp.where(line == 0, top, total)
+                a_hop(k, s, b, h).start()
+                return carry
+
+            return lax.fori_loop(0, 4, pass_on, carry)
+
+        lax.fori_loop(1, chips, step, 0)
+        if k == 0 and layers > 1:
+            prepare_end(1)
+
+    done(load_wkv(0))
+    project(0, (0, 1))
+    for b in range(2):
+        q_hop(0, 0, b).start()
+    go(load_wo(0))
+    if layers > 1:
+        go(load_wkv(1))
+        for pg in range(LANDS):
+            page_in(1, pg).start()
+    for k in range(rings):
+        ring(k)
+    k = rings - 1
+    finish(k)
+    middle(k)
+    gate_up(k, 0, n_gu)
+    down(k, 0, n_dn)
+    close(k)
     out_ref[...] = xs[own, :]
 
 
@@ -428,6 +497,7 @@
         rows = heads * tokens // 2
         ff = w_gate.shape[2] // 2
         both = 2 * tokens
+        rings = 2 * layers
 
         meta = jnp.concatenate([idx_loc.reshape(-1), count_loc.reshape(-1)])
         meta = jnp.broadcast_to(jnp.pad(meta, (0, 128 - meta.shape[0])), (8, 128))
@@ -452,21 +522,22 @@
             in_specs=[vmem] * 6 + [hbm] * 8,
             out_specs=vmem,
             scratch_shapes=[
-                pltpu.VMEM((both, d_model), bf), pltpu.VMEM((both, d_model), bf), pltpu.VMEM((both, width), bf),
-                pltpu.VMEM((both, ff), bf),
-                pltpu.VMEM((chips, 4, hd, rows), bf), pltpu.VMEM((chips + 1, 4, hd + 8, rows), f32), pltpu.VMEM((2, 4, hd + 8, rows), f32),
+                pltpu.VMEM((both, d_model), bf), pltpu.VMEM((both, d_model), bf), pltpu.VMEM((tokens, width), bf), pltpu.VMEM((both, width), bf),
+                pltpu.VMEM((tokens, ff), bf),
+                pltpu.VMEM((2, chips, 2, hd, rows), bf), pltpu.VMEM((2, chips + 1, 2, 2, hd + 8, rows // 2), f32),
+                pltpu.VMEM((2, 2, 2, 2, hd + 8, rows // 2), f32), pltpu.VMEM((2, 2, hd + 8, rows // 2), f32),
                 [pltpu.VMEM((2, pages, page, hd), bf)] * layers, [pltpu.VMEM((2, pages, hd, page), bf)] * layers,
                 pltpu.VMEM((2, tokens, hd), bf), pltpu.VMEM((2, hd, tokens), bf),
                 pltpu.VMEM((2 * slots, page, rows), f32),
-                pltpu.VMEM((2, both, d_model), f32), pltpu.VMEM((2, both, d_model), f32),
+                pltpu.VMEM((2, tokens, d_model), f32), pltpu.VMEM((2, tokens, d_model), f32),
                 pltpu.VMEM((d_model, width), bf), pltpu.VMEM((2, d_model, hd), bf),
                 pltpu.VMEM((PAIRS, 2, d_model, CHUNK), bf), pltpu.VMEM((DOWNS, ff, DOWN), bf),
                 pltpu.VMEM((group, 8, 128), jnp.int32), pltpu.SMEM((group, 128), jnp.int32),
                 pltpu.VMEM((LANDS, 2, 2 * page, hd), bf), pltpu.VMEM((2, 2 * page, hd), f32),
                 pltpu.VMEM((LANDS, page, hd), bf), pltpu.VMEM((LANDS, hd, page), bf),
-                dma((layers, chips, 4)), dma((layers, chips, 4)), dma((layers, chips, 4)), dma((layers, chips + 1, 4)),
+                dma((rings, chips, 2)), dma((rings, chips, 2)), dma((rings, chips, 2, 2)), dma((rings, chips + 1, 2, 2)),
                 dma((LANDS,)), dma((LANDS, 2)), dma((layers, 2)), dma, dma,
-                dma((layers, 2, n_dn)), dma((layers, 2, n_dn)),
+                dma((rings, 2, n_dn)), dma((rings, 2, n_dn)),
                 dma((3,)), dma((2,)), dma((PAIRS, 2)), dma((DOWNS,)),
                 dma((group,)), dma((group,)), dma,
             ],

time: 223 us -> 230 us (1.031)
  Pallas kernels: 214 us -> 221 us
    pallas_call x1, Pallas kernels: 214 us -> 221 us  [per_device(): pl.pallas_call(functools.partial(kernel, (group, slots)), out_shape=jax.S...]
where the time goes in v3:
time: 230 us; the launch traced here: 229 us
  Pallas kernels  221 us (96%)
  local copies, waits for them, and re-layouts  7.16 us (3%)
    pallas_call x1, Pallas kernels, per_device(): pl.pallas_call(functools.partial(kernel, (group, slots)), out_shape=jax.S...  221 us

profile of v3, /device:TPU:21, one launch (start us, length us, event | category | flops | bytes accessed | tf_op | source)
XLA Modules:
  0.0 229.2 jit_solution(1495379075479588832)
XLA Ops:
  0.0 0.8 copy.15
  0.8 0.1 reshape.40
  0.9 0.7 pad_add_fusion
  1.6 0.6 broadcast_in_dim.18.meta_ref
  2.2 1.3 reshape.43.ga_ref
  3.5 1.3 reshape.44.gm_ref
  4.8 0.1 fusion.2
  5.0 0.1 pad_maximum_fusion
  5.0 0.6 tile.20
  5.7 0.8 tile.9.cos_ref
  6.5 221.1 %shard_map.127 = bf16[64,2048]{1,0:T(8,128)(2,1)} custom-call(s32[8,128]{1,0:T(8,128)} %broadcast_in_dim.18.meta_ref, bf16[64,2048]{1,0:T(8,128)(2,1)} %bitcast.9, f32[128,128]{1,0:T(8,128)} %tile.9.cos_ref, f32[128,128]{1,0:T(8,128)} %bitcast.10, f32[2,1,2048]{2,1,0:T(1,128)} %reshape.43.ga_ref, f32[2,1,2048]{2,1,0:T(1,128)} %reshape.44.gm_ref, ...), custom_call_target="tpu_custom_call" | custom-call | tf_op jit(solution)/shard_map/pallas_call | solution.py:519
  227.6 1.7 copy.17
  (3 shorter events, 0.1 us)

commit v4 on v3

--- a/solution.py
+++ b/solution.py
@@ -401,21 +401,27 @@
             return carry
 
         lax.fori_loop(0, 2, home, 0)
+        for b in range(2):
+            q_hop(k, 0, b).wait_recv()
+            q_hop(k, 1, b).start()
 
         def step(s, carry):
-            for b in range(2):
-                q_hop(k, s - 1, b).wait_recv()
-
-                @pl.when(s < chips - 1)
-                def _():
-                    q_hop(k, s, b).start()
-
             def block(b, carry):
                 source = lax.rem(z + jnp.where(b < 1, chips - s, s), chips)
                 put(found.at[b], *attend(layer, qbuf[i, s, b], 2 * source + i, None))
                 return carry
 
             lax.fori_loop(0, 2, block, 0)
+
+            @pl.when(s < chips - 1)
+            def _():
+                for b in range(2):
+                    q_hop(k, s, b).wait_recv()
+
+                    @pl.when(s < chips - 2)
+                    def _():
+                        q_hop(k, s + 1, b).start()
+
             if k > 0:
                 follow(k - 1, s)
             else:

time: 230 us -> 237 us (1.030)
  Pallas kernels: 221 us -> 228 us
    pallas_call x1, Pallas kernels: 221 us -> 228 us  [per_device(): pl.pallas_call(functools.partial(kernel, (group, slots)), out_shape=jax.S...]
where the time goes in v4:
time: 237 us; the launch traced here: 236 us
  Pallas kernels  228 us (96%)
  local copies, waits for them, and re-layouts  7.16 us (3%)
    pallas_call x1, Pallas kernels, per_device(): pl.pallas_call(functools.partial(kernel, (group, slots)), out_shape=jax.S...  228 us

profile of v4, /device:TPU:21, one launch (start us, length us, event | category | flops | bytes accessed | tf_op | source)
XLA Modules:
  0.0 236.1 jit_solution(16019958770278626557)
XLA Ops:
  0.0 0.8 copy.15
  0.8 0.1 reshape.40
  0.9 0.7 pad_add_fusion
  1.6 0.6 broadcast_in_dim.18.meta_ref
  2.2 1.3 reshape.43.ga_ref
  3.5 1.3 reshape.44.gm_ref
  4.8 0.1 fusion.2
  5.0 0.1 pad_maximum_fusion
  5.0 0.6 tile.20
  5.7 0.8 tile.9.cos_ref
  6.5 228.0 %shard_map.127 = bf16[64,2048]{1,0:T(8,128)(2,1)} custom-call(s32[8,128]{1,0:T(8,128)} %broadcast_in_dim.18.meta_ref, bf16[64,2048]{1,0:T(8,128)(2,1)} %bitcast.9, f32[128,128]{1,0:T(8,128)} %tile.9.cos_ref, f32[128,128]{1,0:T(8,128)} %bitcast.10, f32[2,1,2048]{2,1,0:T(1,128)} %reshape.43.ga_ref, f32[2,1,2048]{2,1,0:T(1,128)} %reshape.44.gm_ref, ...), custom_call_target="tpu_custom_call" | custom-call | tf_op jit(solution)/shard_map/pallas_call | solution.py:525
  234.4 1.7 copy.17
  (3 shorter events, 0.1 us)
